TPU v7x, 32 devices: a whole 2x2x4 slice. The times are simulated.
32 devices in a mesh: row: 8 (over z, y), col: 2 (over core), depth: 2 (over x).
Axes of the slice: x: 2, y: 2, z: 4, core: 2. Of those that a mesh axis runs over, the one named last changes fastest.
Arguments:
- student_hidden: bfloat16 [2048, 768], P('row', ('depth', 'col')), may hold values from -16 to 16
- embedding: bfloat16 [50304, 768], P('col', ('depth', 'row')), as said below
- teacher_logits: bfloat16 [2048, 50304], P('row', ('col', 'depth')), may hold values from -24 to 124, as said below
Outputs:
- loss: float32 [2048], P('row')
- peak_logprob: float32 [2048], P('row')
Inputs may be any that keep to these rules, and one draw needn't show every extreme that they name: embedding entries lie within plus or minus 4 / sqrt(768). teacher_logits lie within -24 and 124; each token's logits carry an offset of 0 to 100.
All inputs are finite; a program needn't handle non-finite values.
Results may differ from a plain program's by a relative error of at most 0.0003.
Values may be sent and summed in bfloat16 or wider, within the bound.
A program may use at most 128 MiB of HBM per device.

v0:
```python
import functools

import jax
import jax.numpy as jnp
from jax import lax
from jax.experimental import pallas as pl
from jax.experimental.pallas import tpu as pltpu
from jax.sharding import PartitionSpec as P

MESH = pl.DeviceIdType.MESH
GROUP = 2
TILE = 640
CHUNK = 1280
SKIP = 2
LOW = -1e30


def place(rows, cols, depths):
    r, c, d = lax.axis_index("row"), lax.axis_index("col"), lax.axis_index("depth")
    return r, c, d, r // GROUP, lax.rem(r, GROUP)


def greet(targets):
    barrier = pltpu.get_barrier_semaphore()
    for row, col, depth in targets:
        pl.semaphore_signal(barrier, inc=1, device_id=(row, col, depth), device_id_type=MESH)
    return barrier


def group_peers(rows, cols, depths):
    r, c, d, q, j = place(rows, cols, depths)
    peers = []
    for dj in range(GROUP):
        for dc in range(cols):
            for dd in range(depths):
                if dj or dc or dd:
                    peers.append((q * GROUP + lax.rem(j + dj, GROUP), lax.rem(c + dc, cols), lax.rem(d + dd, depths), dj))
    return peers


def ends(rows, q):
    steps = rows // GROUP
    low, high = q == 0, q == steps - 1
    return low | high, (q == 1) | (q == steps - 2), jnp.where(q * 2 < steps, GROUP, -GROUP)


def as_count(flag):
    return flag.astype(jnp.int32)


def gather_kernel(
    rows, cols, depths, pieces_ref, teacher_ref, hidden_ref, full_ref, other_ref, extra_ref, hid_ref,
    own_sem, first_send, first_recv, right_send, left_send, line_recv, teach_send, teach_recv, extra_send, extra_recv,
    hid_send, hid_recv, far_send, far_recv,
):
    r, c, d, q, j = place(rows, cols, depths)
    steps = rows // GROUP
    count = depths * GROUP
    chunks = full_ref.shape[2] // CHUNK
    kept = chunks - SKIP
    me = d * GROUP + j
    peers = group_peers(rows, cols, depths)
    end, server, inward = ends(rows, q)

    def slot(block, piece):
        return (piece // GROUP) * rows + block * GROUP + lax.rem(piece, GROUP)

    def lanes(t):
        return pl.ds(pl.multiple_of(t * CHUNK, CHUNK), CHUNK)

    barrier = greet([(a, b, e) for a, b, e, _ in peers])

    @pl.when(q + 1 < steps)
    def _():
        pl.semaphore_signal(barrier, inc=1, device_id=(r + GROUP, c, d), device_id_type=MESH)

    @pl.when(q > 0)
    def _():
        pl.semaphore_signal(barrier, inc=1, device_id=(r - GROUP, c, d), device_id_type=MESH)

    pl.semaphore_wait(barrier, len(peers) + as_count(q + 1 < steps) + as_count(q > 0))

    def first(t, off):
        target = lax.rem(me + off, count)
        return pltpu.make_async_remote_copy(
            src_ref=pieces_ref.at[target, :, lanes(t)], dst_ref=full_ref.at[slot(q, me), :, lanes(t)],
            send_sem=first_send.at[t, off], recv_sem=first_recv.at[t, off],
            device_id=(q * GROUP + lax.rem(target, GROUP), c, target // GROUP), device_id_type=MESH,
        )

    def along(block, t, off, right, own=False):
        piece = lax.rem(me + count - off, count)
        at = full_ref.at[slot(block, piece), :, lanes(t)]
        sems = right_send if right else left_send
        return pltpu.make_async_remote_copy(
            src_ref=pieces_ref.at[me, :, lanes(t)] if own else at, dst_ref=at,
            send_sem=sems.at[block, t, off], recv_sem=line_recv.at[block, t, off],
            device_id=(r + GROUP if right else r - GROUP, c, d), device_id_type=MESH,
        )

    def to_right(t):
        return (q + 1 < steps) & ((t < kept) | (q + 2 < steps))

    def to_left(t):
        return (q > 0) & ((t < kept) | (q > 1))

    def both(t, off, own=False):
        @pl.when(to_right(t))
        def _():
            along(q, t, off, True, own).start()

        @pl.when(to_left(t))
        def _():
            along(q, t, off, False, own).start()

    def launch(t, _):
        for off in range(1, count):
            first(t, off).start()
        return 0

    both(0, 0, True)
    lax.fori_loop(0, chunks, launch, 0)
    hids = []
    for n, (a, b, e, dj) in enumerate(peers):
        hids.append(pltpu.make_async_remote_copy(
            src_ref=hidden_ref, dst_ref=hid_ref.at[dj, d * cols + c], send_sem=hid_send.at[n], recv_sem=hid_recv.at[n],
            device_id=(a, b, e), device_id_type=MESH,
        ))
        hids[-1].start()
    pj = lax.rem(j + 1, GROUP)
    cut = kept * CHUNK
    tail = pl.ds(cut, other_ref.shape[0] - cut)

    def teach(n, part):
        return pltpu.make_async_remote_copy(
            src_ref=teacher_ref.at[pj, part], dst_ref=other_ref.at[part], send_sem=teach_send.at[n], recv_sem=teach_recv.at[n],
            device_id=(q * GROUP + pj, c, d), device_id_type=MESH,
        )

    teaches = [teach(0, tail), teach(1, pl.ds(0, cut))]
    for copy in teaches:
        copy.start()

    def extra(n):
        return pltpu.make_async_remote_copy(
            src_ref=teacher_ref.at[j, tail] if n == 0 else other_ref.at[tail], dst_ref=extra_ref.at[n],
            send_sem=extra_send.at[n], recv_sem=extra_recv.at[n], device_id=(r + inward, c, d), device_id_type=MESH,
        )

    far = [pltpu.make_async_remote_copy(
        src_ref=hidden_ref, dst_ref=hid_ref.at[GROUP, d * cols + c], send_sem=far_send.at[0], recv_sem=far_recv.at[0],
        device_id=(r + inward, c, d), device_id_type=MESH,
    )]
    for n, (a, b, e, dj) in enumerate(peers):
        far.append(pltpu.make_async_remote_copy(
            src_ref=hid_ref.at[GROUP, d * cols + c], dst_ref=hid_ref.at[GROUP + dj, d * cols + c],
            send_sem=far_send.at[n + 1], recv_sem=far_recv.at[n + 1], device_id=(a, b, e), device_id_type=MESH,
        ))

    @pl.when(end)
    def _():
        far[0].start()

    own = pltpu.make_async_copy(pieces_ref.at[me], full_ref.at[slot(q, me)], own_sem.at[0])
    own.start()
    own_hid = pltpu.make_async_copy(hidden_ref, hid_ref.at[0, d * cols + c], own_sem.at[1])
    own_hid.start()

    def start_line(t, _):
        @pl.when(t > 0)
        def _():
            both(t, 0, True)

        for off in range(1, count):
            first(t, off).wait_recv()
            both(t, off)
        return 0

    lax.fori_loop(0, chunks, start_line, 0)

    @pl.when(end)
    def _():
        extra(0).start()
        teaches[0].wait_recv()
        extra(1).start()

    @pl.when(server)
    def _():
        far[0].wait_recv()
        for copy in far[1:]:
            copy.start()

    def step(k, _):
        def chunk(t, _):
            wanted = (t < kept) | ~end
            for off in range(count):
                @pl.when((q - k >= 0) & wanted)
                def _():
                    along(q - k, t, off, True).wait_recv()

                    @pl.when(to_right(t))
                    def _():
                        along(q - k, t, off, True).start()

                @pl.when((q + k < steps) & wanted)
                def _():
                    along(q + k, t, off, False).wait_recv()

                    @pl.when(to_left(t))
                    def _():
                        along(q + k, t, off, False).start()

            return 0

        return lax.fori_loop(0, chunks, chunk, 0)

    lax.fori_loop(1, steps, step, 0)

    def settle(block, _):
        def chunk(t, _):
            for off in range(count):
                @pl.when((block <= q) & to_right(t))
                def _():
                    along(block, t, off, True).wait_send()

                @pl.when((block >= q) & to_left(t))
                def _():
                    along(block, t, off, False).wait_send()

            return 0

        return lax.fori_loop(0, chunks, chunk, 0)

    lax.fori_loop(0, steps, settle, 0)

    def settle_first(t, _):
        for off in range(1, count):
            first(t, off).wait_send()
        return 0

    lax.fori_loop(0, chunks, settle_first, 0)
    for copy in hids:
        copy.wait()
    teaches[1].wait()
    teaches[0].wait_send()
    own.wait()
    own_hid.wait()

    @pl.when(end)
    def _():
        far[0].wait_send()
        extra(0).wait_send()
        extra(1).wait_send()

    @pl.when(~end)
    def _():
        teaches[0].wait_recv()

    @pl.when(server)
    def _():
        extra(0).wait_recv()
        extra(1).wait_recv()
        for copy in far[1:]:
            copy.wait()


def gather(rows, cols, depths, pieces, teacher, hidden):
    count, narrow, padded = pieces.shape
    width = teacher.shape[1]
    steps = rows // GROUP
    chunks = padded // CHUNK
    features, tokens = hidden.shape
    peers = GROUP * cols * depths - 1
    dma = pltpu.SemaphoreType.DMA
    any_space = pl.BlockSpec(memory_space=pl.ANY)
    line = (steps, chunks, count)
    return pl.pallas_call(
        functools.partial(gather_kernel, rows, cols, depths),
        out_shape=(
            jax.ShapeDtypeStruct((depths * rows, narrow, padded), pieces.dtype),
            jax.ShapeDtypeStruct((width, tokens), teacher.dtype),
            jax.ShapeDtypeStruct((GROUP, width - (chunks - SKIP) * CHUNK, tokens), teacher.dtype),
            jax.ShapeDtypeStruct((2 * GROUP, depths * cols, features, tokens), hidden.dtype),
        ),
        in_specs=[any_space] * 3,
        out_specs=[any_space] * 4,
        scratch_shapes=[
            dma((2,)), dma((chunks, count)), dma((chunks, count)), dma(line), dma(line), dma(line),
            dma((2,)), dma((2,)), dma((2,)), dma((2,)), dma((peers,)), dma((peers,)), dma((peers + 1,)), dma((peers + 1,)),
        ],
        compiler_params=pltpu.CompilerParams(collective_id=0, has_side_effects=True),
        name="gather",
    )(pieces, teacher, hidden)


def add_terms(full_ref, teacher_refs, hid_ref, acc, start, size, offset=0, sets=range(GROUP)):
    rows = full_ref[:, :, pl.ds(start, size)].reshape(-1, size)
    for n, teacher_ref in zip(sets, teacher_refs):
        hidden = hid_ref[n].reshape(rows.shape[0], -1)
        tokens = hidden.shape[1]
        student = lax.dot_general(rows, hidden, (((0,), (0,)), ((), ())), preferred_element_type=jnp.float32)
        student = student.reshape(size // 8, 8, tokens)
        teacher = teacher_ref[pl.ds(start - offset, size), :].astype(jnp.float32).reshape(size // 8, 8, tokens)
        top = jnp.maximum(acc[n, 0], jnp.max(student, axis=0))
        acc[n, 1] = acc[n, 1] * jnp.exp(acc[n, 0] - top) + jnp.sum(jnp.exp(student - top[None]), axis=0)
        acc[n, 0] = top
        teacher_top = jnp.maximum(acc[n, 2], jnp.max(teacher, axis=0))
        fade = jnp.exp(acc[n, 2] - teacher_top)
        weights = jnp.exp(teacher - teacher_top[None])
        acc[n, 3] = acc[n, 3] * fade + jnp.sum(weights, axis=0)
        acc[n, 4] = acc[n, 4] * fade + jnp.sum(weights * student, axis=0)
        acc[n, 2] = teacher_top


def terms_kernel(flags, full_ref, own_ref, other_ref, extra_ref, hid_ref, out_ref, acc):
    width = other_ref.shape[0]
    cut = width - extra_ref.shape[1]
    for n in range(2 * GROUP):
        for k in range(5):
            acc[n, k] = jnp.full(acc.shape[2:], LOW if k in (0, 2) else 0.0, jnp.float32)
    main = (own_ref.at[0], other_ref)
    extra = tuple(extra_ref.at[n] for n in range(GROUP))

    def tiles(begin, stop, refs, offset, sets):
        whole = (stop - begin) // TILE

        def tile(i, _):
            start = pl.multiple_of(begin + i * TILE, 128)
            add_terms(full_ref, refs, hid_ref, acc, start, TILE, offset, sets)
            return 0

        lax.fori_loop(0, whole, tile, 0)
        if (stop - begin) % TILE:
            add_terms(full_ref, refs, hid_ref, acc, begin + whole * TILE, (stop - begin) % TILE, offset, sets)

    tiles(0, cut, main, 0, range(GROUP))

    @pl.when(flags[1] == 0)
    def _():
        tiles(cut, width, main, 0, range(GROUP))

    @pl.when(flags[2] == 1)
    def _():
        tiles(cut, width, extra, cut, range(GROUP, 2 * GROUP))

    for n in range(2 * GROUP):
        values = merge([acc[n, k] for k in range(5)])
        out_ref[n] = jnp.concatenate(values + [values[0]] * 3, axis=0)


def merge(parts):
    top, total, teacher_top, teacher_total, cross = parts
    peak = jnp.max(top, axis=0, keepdims=True)
    teacher_peak = jnp.max(teacher_top, axis=0, keepdims=True)
    scale = jnp.exp(teacher_top - teacher_peak)
    return [
        peak,
        jnp.sum(total * jnp.exp(top - peak), axis=0, keepdims=True),
        teacher_peak,
        jnp.sum(teacher_total * scale, axis=0, keepdims=True),
        jnp.sum(cross * scale, axis=0, keepdims=True),
    ]


def terms(flags, full, teacher, other, extra, hid):
    tokens = other.shape[1]
    return pl.pallas_call(
        terms_kernel,
        out_shape=jax.ShapeDtypeStruct((2 * GROUP, 8, tokens), jnp.float32),
        grid_spec=pltpu.PrefetchScalarGridSpec(
            num_scalar_prefetch=1,
            grid=(1,),
            in_specs=[
                pl.BlockSpec(full.shape, lambda i, f: (0, 0, 0)),
                pl.BlockSpec((1,) + other.shape, lambda i, f: (f[0], 0, 0)),
                pl.BlockSpec(other.shape, lambda i, f: (0, 0)),
                pl.BlockSpec(extra.shape, lambda i, f: (0, 0, 0)),
                pl.BlockSpec(hid.shape, lambda i, f: (0, 0, 0, 0)),
            ],
            out_specs=pl.BlockSpec((2 * GROUP, 8, tokens), lambda i, f: (0, 0, 0)),
            scratch_shapes=[pltpu.VMEM((2 * GROUP, 5, 8, tokens), jnp.float32)],
        ),
        compiler_params=pltpu.CompilerParams(vmem_limit_bytes=60 * 2**20),
        name="terms",
    )(flags, full, teacher, other, extra, hid)


def combine_kernel(rows, cols, depths, stats_ref, loss_ref, peak_ref, held, send_sem, recv_sem):
    r, c, d, q, j = place(rows, cols, depths)
    end, server, inward = ends(rows, q)
    peers = group_peers(rows, cols, depths)
    near = len(peers)
    group = [(r, c, d, 0)] + peers
    barrier = greet([(a, b, e) for a, b, e, _ in peers])

    @pl.when(end)
    def _():
        greet([(a + inward, b, e) for a, b, e, _ in group])

    @pl.when(server)
    def _():
        greet([(a - inward, b, e) for a, b, e, _ in group])

    pl.semaphore_wait(barrier, near + as_count(end | server) * len(group))

    def send(n, a, b, e, source):
        return pltpu.make_async_remote_copy(
            src_ref=stats_ref.at[source], dst_ref=held.at[n], send_sem=send_sem.at[n], recv_sem=recv_sem.at[n],
            device_id=(a, b, e), device_id_type=MESH,
        )

    copies = [send(n, a, b, e, dj) for n, (a, b, e, dj) in enumerate(peers)]
    far = [send(near + n, a - inward, b, e, GROUP + dj) for n, (a, b, e, dj) in enumerate(group)]

    @pl.when(server)
    def _():
        for copy in far:
            copy.start()

    for copy in copies:
        copy.start()

    @pl.when(~end)
    def _():
        for n in range(len(group)):
            for k in range(5):
                held[near + n, k] = jnp.full(held.shape[2:], LOW if k in (0, 2) else 0.0, jnp.float32)

    for copy in copies:
        copy.wait()

    @pl.when(server)
    def _():
        for copy in far:
            copy.wait_send()

    @pl.when(end)
    def _():
        for copy in far:
            copy.wait_recv()

    blocks = [stats_ref[0]] + [held[n] for n in range(near + len(group))]
    parts = [jnp.concatenate([block[k : k + 1] for block in blocks], axis=0) for k in range(5)]
    peak, total, _, teacher_total, cross = merge(parts)
    norm_log = jnp.log(total)
    loss_ref[...] = peak + norm_log - cross / teacher_total
    peak_ref[...] = -norm_log


def combine(rows, cols, depths, stats):
    tokens = stats.shape[2]
    slots = 2 * GROUP * cols * depths - 1
    vmem = pl.BlockSpec(memory_space=pltpu.VMEM)
    return pl.pallas_call(
        functools.partial(combine_kernel, rows, cols, depths),
        out_shape=(jax.ShapeDtypeStruct((1, tokens), jnp.float32),) * 2,
        in_specs=[vmem],
        out_specs=(vmem, vmem),
        scratch_shapes=[
            pltpu.VMEM((slots, 8, tokens), jnp.float32),
            pltpu.SemaphoreType.DMA((slots,)),
            pltpu.SemaphoreType.DMA((slots,)),
        ],
        compiler_params=pltpu.CompilerParams(collective_id=1, has_side_effects=True),
        name="combine",
    )(stats)


def on_device(rows, cols, depths, student_hidden, embedding, teacher_logits):
    vocab, narrow = embedding.shape
    width = vocab // (depths * GROUP)
    pieces = embedding.T.reshape(narrow, depths * GROUP, width).transpose(1, 0, 2)
    pieces = jnp.pad(pieces, ((0, 0), (0, 0), (0, -width % CHUNK)))
    teacher = teacher_logits.T.reshape(GROUP, width, -1)
    full, other, extra, hid = gather(rows, cols, depths, pieces, teacher, student_hidden.T)
    row = lax.axis_index("row")
    end, server, _ = ends(rows, row // GROUP)
    flags = jnp.stack([lax.rem(row, GROUP), as_count(end), as_count(server)]).astype(jnp.int32)
    loss, peak = combine(rows, cols, depths, terms(flags, full, teacher, other, extra, hid))
    return loss.reshape(-1), peak.reshape(-1)


def solution(mesh):
    sizes = [mesh.shape[name] for name in ("row", "col", "depth")]
    in_specs = (P("row", ("depth", "col")), P("col", ("depth", "row")), P("row", ("col", "depth")))
    out_specs = (P("row"), P("row"))
    return jax.shard_map(
        functools.partial(on_device, *sizes), mesh=mesh, in_specs=in_specs, out_specs=out_specs, check_vma=False
    )
```

profile of v0, /device:TPU:0, one launch (start us, length us, event | category | flops | bytes accessed | tf_op | source)
XLA Modules:
  0.0 161.1 jit_solution(9441544678656728273)
XLA Ops:
  0.7 0.6 pad_add_fusion.flags
  1.3 4.8 %reshape.16 = bf16[48,4,6288]{2,1,0:T(4,128)(2,1)S(1)} reshape(bf16[48,25152]{1,0:T(8,128)(2,1)} %bitcast.16) | data formatting | bytes 4829184 | tf_op jit(solution)/shard_map/reshape | solution.py:472
  6.1 0.2 copy.7
  6.4 1.6 pad.4.pieces_ref
  7.9 116.1 %gather.1 = (bf16[16,48,6400]{2,1,0:T(8,128)(2,1)}, bf16[6288,256]{1,0:T(8,128)(2,1)}, bf16[2,2448,256]{2,1,0:T(8,128)(2,1)}, bf16[4,4,192,256]{3,2,1,0:T(8,128)(2,1)}) custom-call(bf16[4,48,6400]{2,1,0:T(8,128)(2,1)} %pad.4.pieces_ref, bf16[2,6288,256]{2,1,0:T(8,128)(2,1)} %bitcast.13, bf16[192,256]{1,0:T(8,128)(2,1)} %bitcast.17), custom_call_target="tpu_custom_call" | custom-call | tf_op jit(solution)/shard_map/gather/pallas_call | solution.py:277
  124.0 14.5 %terms.1.stats_ref = f32[4,8,256]{2,1,0:T(8,128)} custom-call(s32[3]{0:T(128)} %pad_add_fusion.flags, bf16[16,48,6400]{2,1,0:T(8,128)(2,1)} %get-tuple-element.8.full_ref, bf16[2,6288,256]{2,1,0:T(8,128)(2,1)} %bitcast.14, bf16[6288,256]{1,0:T(8,128)(2,1)} %get-tuple-element.9.other_ref, bf16[2,2448,256]{2,1,0:T(8,128)(2,1)} %get-tuple-element.10.extra_ref, ...), custom_call_target="tpu_custom_call" | custom-call | tf_op jit(solution)/shard_map/terms/pallas_call | solution.py:367
  138.5 20.1 %combine.1 = (f32[1,256]{1,0:T(1,128)}, f32[1,256]{1,0:T(1,128)}) custom-call(f32[4,8,256]{2,1,0:T(8,128)} %terms.1.stats_ref), custom_call_target="tpu_custom_call" | custom-call | tf_op jit(solution)/shard_map/combine/pallas_call | solution.py:454
  158.7 1.2 copy.10
  159.9 1.2 copy.11
where the time goes:
time: 161 us
  Pallas kernels  151 us (94%)
  local copies, waits for them, and re-layouts  9.1 us (6%)
    pallas_call x1, Pallas kernels, gather(): pl.pallas_call(functools.partial(gather_kernel, rows, cols, depths), out_...  116 us
    pallas_call x1, Pallas kernels, combine(): pl.pallas_call(functools.partial(combine_kernel, rows, cols, depths), out...  20.1 us
    pallas_call x1, Pallas kernels, terms(): pl.pallas_call(terms_kernel, out_shape=jax.ShapeDtypeStruct((2 * GROUP, 8...  14.5 us
    reshape x2, local copies, waits for them, and re-layouts, on_device(): embedding.T.reshape(narrow, depths * GROUP, width).transpose(1, 0, 2)  5.09 us

commit v1 on v0

v1 whole, which is shorter than its diff:
```python
import functools

import jax
import jax.numpy as jnp
from jax import lax
from jax.experimental import pallas as pl
from jax.experimental.pallas import tpu as pltpu
from jax.sharding import PartitionSpec as P

MESH = pl.DeviceIdType.MESH
GROUP = 2
LANE = 128
CHUNK = 256
KEPT = 0.64
LOW = -1e30


class Layout:
    def __init__(self, vocab, depths):
        self.half = vocab // depths
        self.stride = vocab // LANE // (depths * GROUP) * LANE
        self.shift = self.half - GROUP * self.stride
        self.last = self.half - (GROUP - 1) * self.stride
        top = self.last + self.shift * (depths - 1)
        self.chunks = -(-top // CHUNK)
        self.width = self.chunks * CHUNK
        self.kept = round(self.chunks * KEPT)
        self.tail = self.stride * (depths * GROUP - 1) + (self.chunks - 1) * CHUNK
        self.edge = (self.chunks - 1) * CHUNK
        assert depths == 2 and self.edge < self.stride and 0 <= self.shift < CHUNK and self.shift % 16 == 0
        assert vocab - self.tail <= CHUNK


def place():
    r, c, d = lax.axis_index("row"), lax.axis_index("col"), lax.axis_index("depth")
    return r, c, d, r // GROUP, lax.rem(r, GROUP)


def ends(rows, q):
    steps = rows // GROUP
    low, high = q == 0, q == steps - 1
    return low | high, (q == 1) | (q == steps - 2), jnp.where(q * 2 < steps, GROUP, -GROUP)


def as_count(flag):
    return flag.astype(jnp.int32)


def loop(begin, stop, body):
    def step(i, _):
        body(i)
        return 0

    lax.fori_loop(begin, stop, step, 0)


def merge(parts):
    top, total, teacher_top, teacher_total, cross = parts
    peak = jnp.max(top, axis=0, keepdims=True)
    teacher_peak = jnp.max(teacher_top, axis=0, keepdims=True)
    scale = jnp.exp(teacher_top - teacher_peak)
    return [
        peak,
        jnp.sum(total * jnp.exp(top - peak), axis=0, keepdims=True),
        teacher_peak,
        jnp.sum(teacher_total * scale, axis=0, keepdims=True),
        jnp.sum(cross * scale, axis=0, keepdims=True),
    ]


def add_terms(full_ref, hid_ref, acc, n, lanes, teacher, valid=None):
    rows = full_ref[:, :, :, lanes].reshape(-1, CHUNK)
    hidden = hid_ref[n].reshape(rows.shape[0], -1)
    tokens = hidden.shape[1]
    student = lax.dot_general(rows, hidden, (((0,), (0,)), ((), ())), preferred_element_type=jnp.float32)
    teacher = teacher.astype(jnp.float32)
    if valid is not None:
        index = lax.broadcasted_iota(jnp.int32, student.shape, 0)
        keep = (index >= valid[0]) & (index < valid[1])
        student = jnp.where(keep, student, LOW)
        teacher = jnp.where(keep, teacher, LOW)
    student = student.reshape(CHUNK // 8, 8, tokens)
    teacher = teacher.reshape(CHUNK // 8, 8, tokens)
    top = jnp.maximum(acc[n, 0], jnp.max(student, axis=0))
    acc[n, 1] = acc[n, 1] * jnp.exp(acc[n, 0] - top) + jnp.sum(jnp.exp(student - top[None]), axis=0)
    acc[n, 0] = top
    teacher_top = jnp.maximum(acc[n, 2], jnp.max(teacher, axis=0))
    fade = jnp.exp(acc[n, 2] - teacher_top)
    weights = jnp.exp(teacher - teacher_top[None])
    acc[n, 3] = acc[n, 3] * fade + jnp.sum(weights, axis=0)
    acc[n, 4] = acc[n, 4] * fade + jnp.sum(weights * student, axis=0)
    acc[n, 2] = teacher_top


def kernel(
    rows, cols, depths, lay, emb_ref, tail_ref, teacher_ref, hidden_ref, loss_ref, peak_ref,
    full_ref, own_ref, other_ref, extra_ref, hid_ref, acc, stats_ref, held_ref,
    own_sem, first_send, first_recv, right_send, left_send, line_recv, teach_send, teach_recv, extra_send, extra_recv,
    hid_send, hid_recv, stats_send, stats_recv,
):
    r, c, d, q, j = place()
    steps = rows // GROUP
    count = depths * GROUP
    me = d * GROUP + j
    chunks, kept, edge = lay.chunks, lay.kept, lay.edge
    end, server, inward = ends(rows, q)
    pj = lax.rem(j + 1, GROUP)
    pr = q * GROUP + pj
    slice_ = d * cols + c
    peers = []
    for dj in range(GROUP):
        for dc in range(cols):
            for dd in range(depths):
                if dj or dc or dd:
                    peers.append((q * GROUP + lax.rem(j + dj, GROUP), lax.rem(c + dc, cols), lax.rem(d + dd, depths), dj))
    group = [(r, c, d, 0)] + peers
    near = len(peers)
    same = [(a, b, e) for a, b, e, dj in peers if dj == 0]

    def lanes(t):
        return pl.ds(pl.multiple_of(t * CHUNK, CHUNK), CHUNK)

    has_head = ~((d > 0) & (j == 0))
    peer_head = ~((d > 0) & (pj == 0))
    has_tail = (d == depths - 1) & (j == GROUP - 1)
    peer_tail = (d == depths - 1) & (pj == GROUP - 1)
    shift = lay.shift * (depths - 1)

    def source(part, at, size):
        begin = jnp.clip(lay.stride * part - lay.shift * d + at, 0, lay.half - size)
        return teacher_ref.at[pl.ds(pl.multiple_of(begin, 16), size)]

    own_body = pltpu.make_async_copy(source(j, shift, lay.last - shift), own_ref.at[pl.ds(shift, lay.last - shift)], own_sem.at[0])
    own_head = pltpu.make_async_copy(source(j, 0, shift), own_ref.at[pl.ds(0, shift)], own_sem.at[1])
    own_tail = pltpu.make_async_copy(source(j, lay.last, shift), own_ref.at[pl.ds(lay.last, shift)], own_sem.at[2])
    own_body.start()

    @pl.when(has_head)
    def _():
        own_head.start()

    @pl.when(has_tail)
    def _():
        own_tail.start()

    own_hid = pltpu.make_async_copy(hidden_ref, hid_ref.at[0, slice_], own_sem.at[3])
    own_hid.start()

    def piece(target, t):
        return emb_ref.at[:, pl.ds(pl.multiple_of(lay.stride * target + t * CHUNK, LANE), CHUNK)]

    own_piece = pltpu.make_async_copy(
        emb_ref.at[:, pl.ds(pl.multiple_of(lay.stride * me, LANE), edge)], full_ref.at[d, r, :, pl.ds(0, edge)], own_sem.at[4]
    )
    own_piece.start()

    def own_edge(source_ref):
        return pltpu.make_async_copy(source_ref, full_ref.at[d, r, :, pl.ds(edge, CHUNK)], own_sem.at[5])

    @pl.when(me < count - 1)
    def _():
        own_edge(piece(me, chunks - 1)).start()

    @pl.when(me == count - 1)
    def _():
        own_edge(tail_ref).start()

    barrier = pltpu.get_barrier_semaphore()

    def greet(row, col, depth):
        pl.semaphore_signal(barrier, inc=1, device_id=(row, col, depth), device_id_type=MESH)

    for a, b, e, _ in peers:
        greet(a, b, e)

    @pl.when(q + 1 < steps)
    def _():
        greet(r + GROUP, c, d)

    @pl.when(q > 0)
    def _():
        greet(r - GROUP, c, d)

    @pl.when(end)
    def _():
        for a, b, e, _ in peers:
            greet(a + inward, b, e)

    @pl.when(server)
    def _():
        for a, b, e, _ in peers:
            greet(a - inward, b, e)

    pl.semaphore_wait(barrier, near * (1 + as_count(end | server)) + as_count(q + 1 < steps) + as_count(q > 0))

    def first(t, off, source_ref):
        target = lax.rem(me + off, count)
        return pltpu.make_async_remote_copy(
            src_ref=source_ref, dst_ref=full_ref.at[d, r, :, lanes(t)], send_sem=first_send.at[0], recv_sem=first_recv.at[t],
            device_id=(q * GROUP + lax.rem(target, GROUP), c, target // GROUP), device_id_type=MESH,
        )

    def first_arrived(t):
        at = full_ref.at[0, pl.ds(0, count - 1), :, lanes(t)]
        return pltpu.make_async_remote_copy(
            src_ref=at, dst_ref=at, send_sem=first_send.at[0], recv_sem=first_recv.at[t], device_id=(pr, c, d), device_id_type=MESH,
        )

    def send_line(source_ref, dst_ref, block, t, right):
        sems = right_send if right else left_send
        return pltpu.make_async_remote_copy(
            src_ref=source_ref, dst_ref=dst_ref, send_sem=sems.at[block], recv_sem=line_recv.at[block, t],
            device_id=(r + GROUP if right else r - GROUP, c, d), device_id_type=MESH,
        )

    def block_at(block, at):
        return full_ref.at[:, pl.ds(pl.multiple_of(block * GROUP, GROUP), GROUP), :, at]

    def along(block, t, right):
        at = block_at(block, lanes(t))
        return send_line(at, at, block, t, right)

    def to_right(t):
        return (q + 1 < steps) & ((t < kept) | (q + 2 < steps))

    def to_left(t):
        return (q > 0) & ((t < kept) | (q > 1))

    def both(t, source_ref, dst_ref):
        @pl.when(to_right(t))
        def _():
            send_line(source_ref, dst_ref, q, t, True).start()

        @pl.when(to_left(t))
        def _():
            send_line(source_ref, dst_ref, q, t, False).start()

    def launch(t):
        for off in range(1, count):
            first(t, off, piece(lax.rem(me + off, count), t)).start()
        both(t, piece(me, t), full_ref.at[d, r, :, lanes(t)])

    loop(0, chunks - 1, launch)
    final = chunks - 1
    for off in range(count):
        target = lax.rem(me + off, count)

        def send(source_ref, off=off):
            if off:
                first(final, off, source_ref).start()
            else:
                both(final, source_ref, full_ref.at[d, r, :, lanes(final)])

        @pl.when(target < count - 1)
        def _():
            send(piece(target, final))

        @pl.when(target == count - 1)
        def _():
            send(tail_ref)

    def give(n, sem, a, b, e, source_ref):
        return pltpu.make_async_remote_copy(
            src_ref=source_ref, dst_ref=hid_ref.at[n, slice_], send_sem=hid_send.at[sem], recv_sem=hid_recv.at[sem],
            device_id=(a, b, e), device_id_type=MESH,
        )

    ways = len(same) + 1
    cross = [give(1, 0, pr, c, d, hidden_ref), None, give(3, 2 * ways, pr, c, d, hid_ref.at[2, slice_])]
    spread = [
        [
            give(n, n * ways + 1 + k, a, b, e, hidden_ref if n == 0 else hid_ref.at[n, slice_])
            for k, (a, b, e) in enumerate(same)
        ]
        for n in range(2 * GROUP)
    ]
    far_hid = give(2, 4 * ways, r + inward, c, d, hidden_ref)
    cross[0].start()
    for copy in spread[0]:
        copy.start()

    body = lay.last - edge

    def teach(t, size=CHUNK, at=0):
        where = pl.multiple_of(t * CHUNK, CHUNK) + at
        return pltpu.make_async_remote_copy(
            src_ref=source(pj, where, size), dst_ref=other_ref.at[pl.ds(where, size)],
            send_sem=teach_send.at[0], recv_sem=teach_recv.at[t], device_id=(pr, c, d), device_id_type=MESH,
        )

    def teach_edge(n, at, size):
        return pltpu.make_async_remote_copy(
            src_ref=source(pj, at, size), dst_ref=other_ref.at[pl.ds(at, size)],
            send_sem=teach_send.at[1 + n], recv_sem=teach_recv.at[chunks + n], device_id=(pr, c, d), device_id_type=MESH,
        )

    def teach_kept():
        teach(0, CHUNK - shift, shift).start()

        @pl.when(peer_head)
        def _():
            teach_edge(0, 0, shift).start()

        loop(1, kept, lambda t: teach(t).start())

    def teach_rest():
        loop(kept, final, lambda t: teach(t).start())
        teach(final, body).start()

        @pl.when(peer_tail)
        def _():
            teach_edge(1, lay.last, shift).start()

    @pl.when(end)
    def _():
        teach_rest()

    teach_kept()

    @pl.when(~end)
    def _():
        teach_rest()

    def teach_first_arrived():
        teach(0, CHUNK - shift, shift).wait_recv()

        @pl.when(has_head)
        def _():
            teach_edge(0, 0, shift).wait_recv()

    def teach_last_arrived():
        teach(final, body).wait_recv()

        @pl.when(has_tail)
        def _():
            teach_edge(1, lay.last, shift).wait_recv()

    def start_line(t):
        first_arrived(t).wait_recv()
        for off in range(1, count):
            sender = lax.rem(me + count - off, count)
            at = full_ref.at[sender // GROUP, q * GROUP + lax.rem(sender, GROUP), :, lanes(t)]
            both(t, at, at)

    loop(0, chunks, start_line)

    cross[0].wait_recv()
    for copy in spread[1]:
        copy.start()

    def extra(n, t, size=CHUNK):
        where = pl.multiple_of(t * CHUNK, CHUNK)
        return pltpu.make_async_remote_copy(
            src_ref=source(j, where, size) if n == 0 else other_ref.at[pl.ds(where, size)],
            dst_ref=extra_ref.at[n, pl.ds(pl.multiple_of(where - kept * CHUNK, CHUNK), size)],
            send_sem=extra_send.at[n], recv_sem=extra_recv.at[n, t - kept], device_id=(r + inward, c, d), device_id_type=MESH,
        )

    def extra_edge(n):
        at = lay.last - kept * CHUNK
        return pltpu.make_async_remote_copy(
            src_ref=source(j, lay.last, shift) if n == 0 else other_ref.at[pl.ds(lay.last, shift)],
            dst_ref=extra_ref.at[n, pl.ds(at, shift)],
            send_sem=extra_send.at[GROUP + n], recv_sem=extra_recv.at[n, chunks - kept],
            device_id=(r + inward, c, d), device_id_type=MESH,
        )

    @pl.when(end)
    def _():
        far_hid.start()

        def pass_on(t):
            teach(t).wait_recv()
            for n in range(GROUP):
                extra(n, t).start()

        loop(kept, final, pass_on)
        teach_last_arrived()
        for n in range(GROUP):
            extra(n, final, body).start()

        @pl.when(has_tail)
        def _():
            for n in range(GROUP):
                extra_edge(n).start()

    def hop(k, t):
        wanted = (t < kept) | ~end

        @pl.when((q - k >= 0) & wanted)
        def _():
            along(q - k, t, True).wait_recv()

            @pl.when(to_right(t))
            def _():
                along(q - k, t, True).start()

        @pl.when((q + k < steps) & wanted)
        def _():
            along(q + k, t, False).wait_recv()

            @pl.when(to_left(t))
            def _():
                along(q + k, t, False).start()

    far = jnp.maximum(q, steps - 1 - q)
    loop(1, far, lambda k: loop(0, chunks, lambda t: hop(k, t)))

    for n in range(2 * GROUP):
        for k in range(5):
            acc[n, k] = jnp.full(acc.shape[2:], LOW if k in (0, 2) else 0.0, jnp.float32)

    def main(t, valid=None):
        at = pl.ds(pl.multiple_of(t * CHUNK, CHUNK), CHUNK)
        for n, ref in enumerate((own_ref, other_ref)):
            add_terms(full_ref, hid_ref, acc, n, at, ref[at, :], valid)

    def more(t, valid=None):
        at = pl.ds(pl.multiple_of(t * CHUNK, CHUNK), CHUNK)
        from_ = pl.ds(pl.multiple_of((t - kept) * CHUNK, CHUNK), CHUNK)
        for n in range(GROUP):
            add_terms(full_ref, hid_ref, acc, GROUP + n, at, extra_ref[n, from_, :], valid)

    hop(far, 0)

    @pl.when(server)
    def _():
        far_hid.wait_recv()
        cross[2].start()
        for copy in spread[2]:
            copy.start()

    own_body.wait()

    @pl.when(has_head)
    def _():
        own_head.wait()

    @pl.when(has_tail)
    def _():
        own_tail.wait()

    own_hid.wait()
    own_piece.wait()
    own_edge(tail_ref).wait()
    for n in range(2):
        for copy in spread[n]:
            copy.wait_recv()
    teach_first_arrived()
    main(0, (jnp.where(has_head, 0, shift), CHUNK))

    def kept_chunk(t):
        hop(far, t)
        teach(t).wait_recv()
        main(t)

    half = kept // 2
    loop(1, half, kept_chunk)

    @pl.when(server)
    def _():
        cross[2].wait_recv()
        for copy in spread[3]:
            copy.start()

    loop(half, kept, kept_chunk)

    @pl.when(server)
    def _():
        for n in range(2, 4):
            for copy in spread[n]:
                copy.wait_recv()

    limit = (0, jnp.where(j == 0, lay.stride, lay.last + lay.shift * d) - edge)

    @pl.when(~end)
    def _():
        def rest_chunk(t):
            hop(far, t)

            @pl.when(server)
            def _():
                for n in range(GROUP):
                    extra(n, t).wait_recv()
                more(t)

            teach(t).wait_recv()
            main(t)

        loop(kept, final, rest_chunk)
        hop(far, final)

    def close(n):
        values = merge([acc[n, k] for k in range(5)])
        stats_ref[n] = jnp.concatenate(values + [values[0]] * 3, axis=0)

    def tell(n, a, b, e, source_set):
        return pltpu.make_async_remote_copy(
            src_ref=stats_ref.at[source_set], dst_ref=held_ref.at[n], send_sem=stats_send.at[n], recv_sem=stats_recv.at[n],
            device_id=(a, b, e), device_id_type=MESH,
        )

    copies = [tell(n, a, b, e, dj) for n, (a, b, e, dj) in enumerate(peers)]
    far_copies = [tell(near + n, a - inward, b, e, GROUP + dj) for n, (a, b, e, dj) in enumerate(group)]

    @pl.when(server)
    def _():
        for n in range(GROUP):
            extra(n, final, body).wait_recv()

        @pl.when(has_tail)
        def _():
            for n in range(GROUP):
                extra_edge(n).wait_recv()

        more(final, limit)
        for n in range(GROUP, 2 * GROUP):
            close(n)
        for copy in far_copies:
            copy.start()

    @pl.when(~end)
    def _():
        teach_last_arrived()
        main(final, limit)

    for n in range(GROUP):
        close(n)
    for copy in copies:
        copy.start()

    @pl.when(~end)
    def _():
        for n in range(len(group)):
            for k in range(5):
                held_ref[near + n, k] = jnp.full(held_ref.shape[2:], LOW if k in (0, 2) else 0.0, jnp.float32)

    def settle(block):
        def sent(right, size):
            at = block_at(block, pl.ds(0, size))
            send_line(at, at, block, 0, right).wait_send()

        @pl.when((block <= q) & (q + 2 < steps))
        def _():
            sent(True, lay.width)

        @pl.when((block <= q) & (q + 2 == steps))
        def _():
            sent(True, kept * CHUNK)

        @pl.when((block >= q) & (q > 1))
        def _():
            sent(False, lay.width)

        @pl.when((block >= q) & (q == 1))
        def _():
            sent(False, kept * CHUNK)

    loop(0, steps, settle)
    sent_pieces = full_ref.at[0, pl.ds(0, count - 1)]
    pltpu.make_async_remote_copy(
        src_ref=sent_pieces, dst_ref=sent_pieces, send_sem=first_send.at[0], recv_sem=first_recv.at[0],
        device_id=(pr, c, d), device_id_type=MESH,
    ).wait_send()
    cross[0].wait_send()
    for n in range(2):
        for copy in spread[n]:
            copy.wait_send()
    whole = other_ref.at[pl.ds(shift, lay.last - shift)]
    pltpu.make_async_remote_copy(
        src_ref=whole, dst_ref=whole, send_sem=teach_send.at[0], recv_sem=teach_recv.at[0], device_id=(pr, c, d), device_id_type=MESH,
    ).wait_send()

    @pl.when(peer_head)
    def _():
        teach_edge(0, 0, shift).wait_send()

    @pl.when(peer_tail)
    def _():
        teach_edge(1, lay.last, shift).wait_send()

    @pl.when(end)
    def _():
        far_hid.wait_send()
        part = other_ref.at[pl.ds(kept * CHUNK, lay.last - kept * CHUNK)]
        for n in range(GROUP):
            pltpu.make_async_remote_copy(
                src_ref=part, dst_ref=part, send_sem=extra_send.at[n], recv_sem=extra_recv.at[n, 0],
                device_id=(pr, c, d), device_id_type=MESH,
            ).wait_send()

        @pl.when(has_tail)
        def _():
            for n in range(GROUP):
                extra_edge(n).wait_send()

    @pl.when(server)
    def _():
        cross[2].wait_send()
        for n in range(2, 4):
            for copy in spread[n]:
                copy.wait_send()
        for copy in far_copies:
            copy.wait_send()

    for copy in copies:
        copy.wait()

    @pl.when(end)
    def _():
        for copy in far_copies:
            copy.wait_recv()

    blocks = [stats_ref[0]] + [held_ref[n] for n in range(near + len(group))]
    parts = [jnp.concatenate([block[k : k + 1] for block in blocks], axis=0) for k in range(5)]
    peak, total, _, teacher_total, cross_sum = merge(parts)
    norm_log = jnp.log(total)
    loss_ref[...] = peak + norm_log - cross_sum / teacher_total
    peak_ref[...] = -norm_log


def on_device(rows, cols, depths, student_hidden, embedding, teacher_logits):
    vocab, narrow = embedding.shape
    lay = Layout(vocab, depths)
    table = embedding.T
    tail = jnp.pad(embedding.T[:, lay.tail :], ((0, 0), (0, lay.tail + CHUNK - vocab)))
    hidden = student_hidden.T
    features, tokens = hidden.shape
    steps = rows // GROUP
    peers = GROUP * cols * depths - 1
    slots = 2 * GROUP * cols * depths - 1
    ways = cols * depths
    chunks = lay.chunks
    dma = pltpu.SemaphoreType.DMA
    any_space = pl.BlockSpec(memory_space=pl.ANY)
    vmem = pl.BlockSpec(memory_space=pltpu.VMEM)
    dtype = embedding.dtype
    loss, peak = pl.pallas_call(
        functools.partial(kernel, rows, cols, depths, lay),
        out_shape=(jax.ShapeDtypeStruct((1, tokens), jnp.float32),) * 2,
        in_specs=[any_space] * 4,
        out_specs=(vmem, vmem),
        scratch_shapes=[
            pltpu.VMEM((depths, rows, narrow, lay.width), dtype),
            pltpu.VMEM((lay.width, tokens), teacher_logits.dtype),
            pltpu.VMEM((lay.width, tokens), teacher_logits.dtype),
            pltpu.VMEM((GROUP, lay.width - lay.kept * CHUNK, tokens), teacher_logits.dtype),
            pltpu.VMEM((2 * GROUP, depths * cols, features, tokens), hidden.dtype),
            pltpu.VMEM((2 * GROUP, 5, 8, tokens), jnp.float32),
            pltpu.VMEM((2 * GROUP, 8, tokens), jnp.float32),
            pltpu.VMEM((slots, 8, tokens), jnp.float32),
            dma((6,)), dma((1,)), dma((chunks,)), dma((steps,)), dma((steps,)), dma((steps, chunks)),
            dma((3,)), dma((chunks + 2,)), dma((2 * GROUP,)), dma((GROUP, chunks - lay.kept + 1)),
            dma((4 * ways + 1,)), dma((4 * ways + 1,)), dma((slots,)), dma((slots,)),
        ],
        compiler_params=pltpu.CompilerParams(collective_id=0, has_side_effects=True, vmem_limit_bytes=60 * 2**20),
        name="distill",
    )(table, tail, teacher_logits.T, hidden)
    return loss.reshape(-1), peak.reshape(-1)


def solution(mesh):
    sizes = [mesh.shape[name] for name in ("row", "col", "depth")]
    in_specs = (P("row", ("depth", "col")), P("col", ("depth", "row")), P("row", ("col", "depth")))
    out_specs = (P("row"), P("row"))
    return jax.shard_map(
        functools.partial(on_device, *sizes), mesh=mesh, in_specs=in_specs, out_specs=out_specs, check_vma=False
    )
```

time: 161 us -> 137 us (0.85)
  Pallas kernels: 151 us -> 132 us
  local copies, waits for them, and re-layouts: 9.1 us -> 3.78 us
    pallas_call x3 -> x1, Pallas kernels: 151 us -> 132 us  [on_device(): pl.pallas_call(functools.partial(kernel, rows, cols, depths, lay), out_sh...]
    reshape x2 -> x0, local copies, waits for them, and re-layouts: 5.09 us -> none  [on_device(): embedding.T.reshape(narrow, depths * GROUP, width).transpose(1, 0, 2)]
where the time goes in v1:
time: 137 us; the launch traced here: 136 us
  Pallas kernels  132 us (96%)
  local copies, waits for them, and re-layouts  3.78 us (3%)
    pallas_call x1, Pallas kernels, on_device(): pl.pallas_call(functools.partial(kernel, rows, cols, depths, lay), out_sh...  132 us

profile of v1, /device:TPU:0, one launch (start us, length us, event | category | flops | bytes accessed | tf_op | source)
XLA Modules:
  0.0 136.4 jit_solution(13278992155494582880)
XLA Ops:
  0.6 0.7 slice.4
  1.4 0.6 pad.4.tail_ref
  2.0 132.0 %distill.1 = (f32[1,256]{1,0:T(1,128)}, f32[1,256]{1,0:T(1,128)}) custom-call(bf16[48,25152]{1,0:T(8,128)(2,1)} %bitcast.7, bf16[48,256]{1,0:T(8,128)(2,1)} %pad.4.tail_ref, bf16[12576,256]{1,0:T(8,128)(2,1)} %bitcast.5, bf16[192,256]{1,0:T(8,128)(2,1)} %bitcast.8), custom_call_target="tpu_custom_call" | custom-call | tf_op jit(solution)/shard_map/distill/pallas_call | solution.py:638
  134.0 1.2 copy.7
  135.2 1.2 copy.8

commit v2 on v1

--- a/solution.py
+++ b/solution.py
@@ -93,8 +93,8 @@
 
 
 def kernel(
-    rows, cols, depths, lay, emb_ref, tail_ref, teacher_ref, hidden_ref, loss_ref, peak_ref,
-    full_ref, own_ref, other_ref, extra_ref, hid_ref, acc, stats_ref, held_ref,
+    rows, cols, depths, lay, emb_ref, teacher_ref, hidden_ref, sums_ref,
+    table_ref, tail_ref, full_ref, own_ref, other_ref, extra_ref, hid_ref, acc, stats_ref, held_ref,
     own_sem, first_send, first_recv, right_send, left_send, line_recv, teach_send, teach_recv, extra_send, extra_recv,
     hid_send, hid_recv, stats_send, stats_recv,
 ):
@@ -120,6 +120,22 @@
     def lanes(t):
         return pl.ds(pl.multiple_of(t * CHUNK, CHUNK), CHUNK)
 
+    barrier = pltpu.get_barrier_semaphore()
+
+    def greet(row, col, depth):
+        pl.semaphore_signal(barrier, inc=1, device_id=(row, col, depth), device_id_type=MESH)
+
+    for a, b, e, _ in peers:
+        greet(a, b, e)
+
+    @pl.when(q + 1 < steps)
+    def _():
+        greet(r + GROUP, c, d)
+
+    @pl.when(q > 0)
+    def _():
+        greet(r - GROUP, c, d)
+
     has_head = ~((d > 0) & (j == 0))
     peer_head = ~((d > 0) & (pj == 0))
     has_tail = (d == depths - 1) & (j == GROUP - 1)
@@ -133,6 +149,8 @@
     own_body = pltpu.make_async_copy(source(j, shift, lay.last - shift), own_ref.at[pl.ds(shift, lay.last - shift)], own_sem.at[0])
     own_head = pltpu.make_async_copy(source(j, 0, shift), own_ref.at[pl.ds(0, shift)], own_sem.at[1])
     own_tail = pltpu.make_async_copy(source(j, lay.last, shift), own_ref.at[pl.ds(lay.last, shift)], own_sem.at[2])
+    load = pltpu.make_async_copy(emb_ref, table_ref, own_sem.at[6])
+    load.start()
     own_body.start()
 
     @pl.when(has_head)
@@ -147,16 +165,21 @@
     own_hid.start()
 
     def piece(target, t):
-        return emb_ref.at[:, pl.ds(pl.multiple_of(lay.stride * target + t * CHUNK, LANE), CHUNK)]
+        return table_ref.at[:, pl.ds(pl.multiple_of(lay.stride * target + t * CHUNK, LANE), CHUNK)]
 
     own_piece = pltpu.make_async_copy(
-        emb_ref.at[:, pl.ds(pl.multiple_of(lay.stride * me, LANE), edge)], full_ref.at[d, r, :, pl.ds(0, edge)], own_sem.at[4]
+        table_ref.at[:, pl.ds(pl.multiple_of(lay.stride * me, LANE), edge)], full_ref.at[d, r, :, pl.ds(0, edge)], own_sem.at[4]
     )
-    own_piece.start()
 
     def own_edge(source_ref):
         return pltpu.make_async_copy(source_ref, full_ref.at[d, r, :, pl.ds(edge, CHUNK)], own_sem.at[5])
 
+    load.wait()
+    left = table_ref.shape[1] - lay.tail
+    tail_ref[:, :left] = table_ref[:, lay.tail :]
+    tail_ref[:, left:] = jnp.zeros((tail_ref.shape[0], CHUNK - left), tail_ref.dtype)
+    own_piece.start()
+
     @pl.when(me < count - 1)
     def _():
         own_edge(piece(me, chunks - 1)).start()
@@ -165,33 +188,7 @@
     def _():
         own_edge(tail_ref).start()
 
-    barrier = pltpu.get_barrier_semaphore()
-
-    def greet(row, col, depth):
-        pl.semaphore_signal(barrier, inc=1, device_id=(row, col, depth), device_id_type=MESH)
-
-    for a, b, e, _ in peers:
-        greet(a, b, e)
-
-    @pl.when(q + 1 < steps)
-    def _():
-        greet(r + GROUP, c, d)
-
-    @pl.when(q > 0)
-    def _():
-        greet(r - GROUP, c, d)
-
-    @pl.when(end)
-    def _():
-        for a, b, e, _ in peers:
-            greet(a + inward, b, e)
-
-    @pl.when(server)
-    def _():
-        for a, b, e, _ in peers:
-            greet(a - inward, b, e)
-
-    pl.semaphore_wait(barrier, near * (1 + as_count(end | server)) + as_count(q + 1 < steps) + as_count(q > 0))
+    pl.semaphore_wait(barrier, near + as_count(q + 1 < steps) + as_count(q > 0))
 
     def first(t, off, source_ref):
         target = lax.rem(me + off, count)
@@ -234,30 +231,6 @@
         @pl.when(to_left(t))
         def _():
             send_line(source_ref, dst_ref, q, t, False).start()
-
-    def launch(t):
-        for off in range(1, count):
-            first(t, off, piece(lax.rem(me + off, count), t)).start()
-        both(t, piece(me, t), full_ref.at[d, r, :, lanes(t)])
-
-    loop(0, chunks - 1, launch)
-    final = chunks - 1
-    for off in range(count):
-        target = lax.rem(me + off, count)
-
-        def send(source_ref, off=off):
-            if off:
-                first(final, off, source_ref).start()
-            else:
-                both(final, source_ref, full_ref.at[d, r, :, lanes(final)])
-
-        @pl.when(target < count - 1)
-        def _():
-            send(piece(target, final))
-
-        @pl.when(target == count - 1)
-        def _():
-            send(tail_ref)
 
     def give(n, sem, a, b, e, source_ref):
         return pltpu.make_async_remote_copy(
@@ -275,10 +248,45 @@
         for n in range(2 * GROUP)
     ]
     far_hid = give(2, 4 * ways, r + inward, c, d, hidden_ref)
+    @pl.when(end)
+    def _():
+        far_hid.start()
+
+    def launch(t):
+        for off in range(1, count):
+            first(t, off, piece(lax.rem(me + off, count), t)).start()
+        both(t, piece(me, t), full_ref.at[d, r, :, lanes(t)])
+
+    loop(0, chunks - 1, launch)
+    final = chunks - 1
+    for off in range(count):
+        target = lax.rem(me + off, count)
+
+        def send(source_ref, off=off):
+            if off:
+                first(final, off, source_ref).start()
+            else:
+                both(final, source_ref, full_ref.at[d, r, :, lanes(final)])
+
+        @pl.when(target < count - 1)
+        def _():
+            send(piece(target, final))
+
+        @pl.when(target == count - 1)
+        def _():
+            send(tail_ref)
+
     cross[0].start()
     for copy in spread[0]:
         copy.start()
 
+    @pl.when(server)
+    def _():
+        far_hid.wait_recv()
+        cross[2].start()
+        for copy in spread[2]:
+            copy.start()
+
     body = lay.last - edge
 
     def teach(t, size=CHUNK, at=0):
@@ -310,16 +318,6 @@
         @pl.when(peer_tail)
         def _():
             teach_edge(1, lay.last, shift).start()
-
-    @pl.when(end)
-    def _():
-        teach_rest()
-
-    teach_kept()
-
-    @pl.when(~end)
-    def _():
-        teach_rest()
 
     def teach_first_arrived():
         teach(0, CHUNK - shift, shift).wait_recv()
@@ -344,9 +342,25 @@
 
     loop(0, chunks, start_line)
 
+    @pl.when(end)
+    def _():
+        teach_rest()
+
+    teach_kept()
+
+    @pl.when(~end)
+    def _():
+        teach_rest()
+
     cross[0].wait_recv()
     for copy in spread[1]:
         copy.start()
+
+    @pl.when(server)
+    def _():
+        cross[2].wait_recv()
+        for copy in spread[3]:
+            copy.start()
 
     def extra(n, t, size=CHUNK):
         where = pl.multiple_of(t * CHUNK, CHUNK)
@@ -367,8 +381,6 @@
 
     @pl.when(end)
     def _():
-        far_hid.start()
-
         def pass_on(t):
             teach(t).wait_recv()
             for n in range(GROUP):
@@ -422,14 +434,6 @@
             add_terms(full_ref, hid_ref, acc, GROUP + n, at, extra_ref[n, from_, :], valid)
 
     hop(far, 0)
-
-    @pl.when(server)
-    def _():
-        far_hid.wait_recv()
-        cross[2].start()
-        for copy in spread[2]:
-            copy.start()
-
     own_body.wait()
 
     @pl.when(has_head)
@@ -454,16 +458,7 @@
         teach(t).wait_recv()
         main(t)
 
-    half = kept // 2
-    loop(1, half, kept_chunk)
-
-    @pl.when(server)
-    def _():
-        cross[2].wait_recv()
-        for copy in spread[3]:
-            copy.start()
-
-    loop(half, kept, kept_chunk)
+    loop(1, kept, kept_chunk)
 
     @pl.when(server)
     def _():
@@ -614,16 +609,12 @@
     blocks = [stats_ref[0]] + [held_ref[n] for n in range(near + len(group))]
     parts = [jnp.concatenate([block[k : k + 1] for block in blocks], axis=0) for k in range(5)]
     peak, total, _, teacher_total, cross_sum = merge(parts)
-    norm_log = jnp.log(total)
-    loss_ref[...] = peak + norm_log - cross_sum / teacher_total
-    peak_ref[...] = -norm_log
+    sums_ref[...] = jnp.concatenate([peak, total, teacher_total, cross_sum] + [peak] * 4, axis=0)
 
 
 def on_device(rows, cols, depths, student_hidden, embedding, teacher_logits):
     vocab, narrow = embedding.shape
     lay = Layout(vocab, depths)
-    table = embedding.T
-    tail = jnp.pad(embedding.T[:, lay.tail :], ((0, 0), (0, lay.tail + CHUNK - vocab)))
     hidden = student_hidden.T
     features, tokens = hidden.shape
     steps = rows // GROUP
@@ -635,12 +626,14 @@
     any_space = pl.BlockSpec(memory_space=pl.ANY)
     vmem = pl.BlockSpec(memory_space=pltpu.VMEM)
     dtype = embedding.dtype
-    loss, peak = pl.pallas_call(
+    sums = pl.pallas_call(
         functools.partial(kernel, rows, cols, depths, lay),
-        out_shape=(jax.ShapeDtypeStruct((1, tokens), jnp.float32),) * 2,
-        in_specs=[any_space] * 4,
-        out_specs=(vmem, vmem),
+        out_shape=jax.ShapeDtypeStruct((8, tokens), jnp.float32),
+        in_specs=[any_space] * 3,
+        out_specs=vmem,
         scratch_shapes=[
+            pltpu.VMEM((narrow, vocab), dtype),
+            pltpu.VMEM((narrow, CHUNK), dtype),
             pltpu.VMEM((depths, rows, narrow, lay.width), dtype),
             pltpu.VMEM((lay.width, tokens), teacher_logits.dtype),
             pltpu.VMEM((lay.width, tokens), teacher_logits.dtype),
@@ -649,14 +642,15 @@
             pltpu.VMEM((2 * GROUP, 5, 8, tokens), jnp.float32),
             pltpu.VMEM((2 * GROUP, 8, tokens), jnp.float32),
             pltpu.VMEM((slots, 8, tokens), jnp.float32),
-            dma((6,)), dma((1,)), dma((chunks,)), dma((steps,)), dma((steps,)), dma((steps, chunks)),
+            dma((7,)), dma((1,)), dma((chunks,)), dma((steps,)), dma((steps,)), dma((steps, chunks)),
             dma((3,)), dma((chunks + 2,)), dma((2 * GROUP,)), dma((GROUP, chunks - lay.kept + 1)),
             dma((4 * ways + 1,)), dma((4 * ways + 1,)), dma((slots,)), dma((slots,)),
         ],
         compiler_params=pltpu.CompilerParams(collective_id=0, has_side_effects=True, vmem_limit_bytes=60 * 2**20),
         name="distill",
-    )(table, tail, teacher_logits.T, hidden)
-    return loss.reshape(-1), peak.reshape(-1)
+    )(embedding.T, teacher_logits.T, hidden)
+    norm_log = jnp.log(sums[1])
+    return sums[0] + norm_log - sums[3] / sums[2], -norm_log
 
 
 def solution(mesh):

time: 137 us -> 122 us (0.89)
  Pallas kernels: 132 us -> 120 us
  local copies, waits for them, and re-layouts: 3.78 us -> 0 us
  other arithmetic: 0 us -> 1.42 us
    pallas_call x1, Pallas kernels: 132 us -> 120 us  [on_device(): pl.pallas_call(functools.partial(kernel, rows, cols, depths, lay), out_sh...]
    unnamed x2 -> x0, local copies, waits for them, and re-layouts: 2.43 us -> none
    neg x0 -> x1, other arithmetic: none -> 1.42 us  [on_device(): return (sums[0] + norm_log - sums[3] / sums[2], -norm_log)]
where the time goes in v2:
time: 122 us
  Pallas kernels  120 us (98%)
  other arithmetic  1.42 us (1%)
    pallas_call x1, Pallas kernels, on_device(): pl.pallas_call(functools.partial(kernel, rows, cols, depths, lay), out_sh...  120 us

profile of v2, /device:TPU:0, one launch (start us, length us, event | category | flops | bytes accessed | tf_op | source)
XLA Modules:
  0.0 122.2 jit_solution(11381795246443002933)
XLA Ops:
  0.6 120.1 %distill.1 = f32[8,256]{1,0:T(8,128)} custom-call(bf16[48,25152]{1,0:T(8,128)(2,1)} %bitcast.6, bf16[12576,256]{1,0:T(8,128)(2,1)} %bitcast.5, bf16[192,256]{1,0:T(8,128)(2,1)} %bitcast.7), custom_call_target="tpu_custom_call" | custom-call | tf_op jit(solution)/shard_map/distill/pallas_call | solution.py:629
  120.8 1.4 %fusion = (f32[1,256]{1,0:T(1,128)}, f32[1,256]{1,0:T(1,128)}) fusion(f32[8,256]{1,0:T(8,128)} %distill.1), kind=kLoop, calls=%fused_computation.2 | loop fusion | flops 1024 | bytes 6144 | tf_op jit(solution)/shard_map/neg | solution.py:653

commit v3 on v2

v3 whole, which is shorter than its diff:
```python
import functools

import jax
import jax.numpy as jnp
from jax import lax
from jax.experimental import pallas as pl
from jax.experimental.pallas import tpu as pltpu
from jax.sharding import PartitionSpec as P

MESH = pl.DeviceIdType.MESH
GROUP = 2
LANE = 128
CHUNK = 512
KEPT = 0.64
LOW = -1e30


class Layout:
    def __init__(self, vocab, depths):
        self.half = vocab // depths
        self.stride = vocab // LANE // (depths * GROUP) * LANE
        self.shift = self.half - GROUP * self.stride
        self.last = self.half - (GROUP - 1) * self.stride
        self.edge = (self.stride - LANE) // CHUNK * CHUNK
        self.whole = self.edge // CHUNK
        self.plain = self.stride - self.edge
        self.rest = self.plain + LANE // 2
        self.kept = round(self.stride / CHUNK * KEPT)
        assert depths == 2 and 0 <= self.shift < CHUNK and self.shift % 16 == 0
        assert self.last + self.shift <= self.stride + LANE // 2 and self.plain % LANE == 0
        assert vocab <= self.stride * depths * GROUP + LANE // 2


def place():
    r, c, d = lax.axis_index("row"), lax.axis_index("col"), lax.axis_index("depth")
    return r, c, d, r // GROUP, lax.rem(r, GROUP)


def ends(rows, q):
    steps = rows // GROUP
    low, high = q == 0, q == steps - 1
    return low | high, (q == 1) | (q == steps - 2), jnp.where(q * 2 < steps, GROUP, -GROUP)


def as_count(flag):
    return flag.astype(jnp.int32)


def loop(begin, stop, body):
    def step(i, _):
        body(i)
        return 0

    lax.fori_loop(begin, stop, step, 0)


def merge(parts):
    top, total, teacher_top, teacher_total, cross = parts
    peak = jnp.max(top, axis=0, keepdims=True)
    teacher_peak = jnp.max(teacher_top, axis=0, keepdims=True)
    scale = jnp.exp(teacher_top - teacher_peak)
    return [
        peak,
        jnp.sum(total * jnp.exp(top - peak), axis=0, keepdims=True),
        teacher_peak,
        jnp.sum(teacher_total * scale, axis=0, keepdims=True),
        jnp.sum(cross * scale, axis=0, keepdims=True),
    ]


def add_terms(rows, hid_ref, acc, n, teacher, valid=None):
    size = rows.shape[1]
    hidden = hid_ref[n].reshape(rows.shape[0], -1)
    tokens = hidden.shape[1]
    student = lax.dot_general(rows, hidden, (((0,), (0,)), ((), ())), preferred_element_type=jnp.float32)
    teacher = teacher.astype(jnp.float32)
    if valid is not None:
        index = lax.broadcasted_iota(jnp.int32, student.shape, 0)
        keep = (index >= valid[0]) & (index < valid[1])
        student = jnp.where(keep, student, LOW)
        teacher = jnp.where(keep, teacher, LOW)
    student = student.reshape(size // 8, 8, tokens)
    teacher = teacher.reshape(size // 8, 8, tokens)
    top = jnp.maximum(acc[n, 0], jnp.max(student, axis=0))
    acc[n, 1] = acc[n, 1] * jnp.exp(acc[n, 0] - top) + jnp.sum(jnp.exp(student - top[None]), axis=0)
    acc[n, 0] = top
    teacher_top = jnp.maximum(acc[n, 2], jnp.max(teacher, axis=0))
    fade = jnp.exp(acc[n, 2] - teacher_top)
    weights = jnp.exp(teacher - teacher_top[None])
    acc[n, 3] = acc[n, 3] * fade + jnp.sum(weights, axis=0)
    acc[n, 4] = acc[n, 4] * fade + jnp.sum(weights * student, axis=0)
    acc[n, 2] = teacher_top


def kernel(
    rows, cols, depths, lay, emb_ref, teacher_ref, hidden_ref, sums_ref,
    table_ref, pack_ref, full_ref, half_ref, own_ref, other_ref, extra_ref, hid_ref, acc, stats_ref, held_ref,
    own_sem, first_send, first_recv, right_send, left_send, line_recv, teach_send, teach_recv, extra_send, extra_recv,
    hid_send, hid_recv, stats_send, stats_recv,
):
    r, c, d, q, j = place()
    steps = rows // GROUP
    count = depths * GROUP
    me = d * GROUP + j
    kept, whole, edge = lay.kept, lay.whole, lay.edge
    narrow = table_ref.shape[0]
    packed = narrow // 2
    end, server, inward = ends(rows, q)
    pj = lax.rem(j + 1, GROUP)
    pr = q * GROUP + pj
    slice_ = d * cols + c
    peers = []
    for dj in range(GROUP):
        for dc in range(cols):
            for dd in range(depths):
                if dj or dc or dd:
                    peers.append((q * GROUP + lax.rem(j + dj, GROUP), lax.rem(c + dc, cols), lax.rem(d + dd, depths), dj))
    group = [(r, c, d, 0)] + peers
    near = len(peers)
    same = [(a, b, e) for a, b, e, dj in peers if dj == 0]

    barrier = pltpu.get_barrier_semaphore()

    def greet(row, col, depth):
        pl.semaphore_signal(barrier, inc=1, device_id=(row, col, depth), device_id_type=MESH)

    @pl.when(q + 1 < steps)
    def _():
        greet(r + GROUP, c, d)

    @pl.when(q > 0)
    def _():
        greet(r - GROUP, c, d)

    for a, b, e, _ in peers:
        greet(a, b, e)

    def remote(source_ref, dst_ref, send_sem, recv_sem, device):
        return pltpu.make_async_remote_copy(
            src_ref=source_ref, dst_ref=dst_ref, send_sem=send_sem, recv_sem=recv_sem, device_id=device, device_id_type=MESH
        )

    load = pltpu.make_async_copy(emb_ref, table_ref, own_sem.at[0])
    load.start()
    load.wait()
    for target in range(count):
        part = table_ref[:, lay.stride * (target + 1) : lay.stride * (target + 1) + LANE // 2]
        pack_ref[target] = jnp.concatenate([part[:packed], part[packed:]], axis=1)

    def span(t):
        return pl.multiple_of(t * CHUNK, CHUNK), CHUNK, t, narrow

    ends_of = ((edge, lay.plain, whole, narrow), (lay.stride, LANE, whole + 1, packed))

    def piece(target, cut):
        first_lane, size, index, height = cut
        if height != narrow:
            return pack_ref.at[target]
        return table_ref.at[:, pl.ds(pl.multiple_of(lay.stride * target + first_lane, LANE), size)]

    def slot(depth, row, cut):
        first_lane, size, _, height = cut
        return full_ref.at[depth, row, :, pl.ds(first_lane, size)] if height == narrow else half_ref.at[depth, row]

    def block_at(block, cut):
        first_lane, size, _, height = cut
        row = pl.ds(pl.multiple_of(block * GROUP, GROUP), GROUP)
        return full_ref.at[:, row, :, pl.ds(first_lane, size)] if height == narrow else half_ref.at[:, row]

    own_piece = pltpu.make_async_copy(
        table_ref.at[:, pl.ds(pl.multiple_of(lay.stride * me, LANE), lay.stride)],
        full_ref.at[d, r], own_sem.at[1],
    )
    own_half = pltpu.make_async_copy(pack_ref.at[me], slot(d, r, ends_of[1]), own_sem.at[2])

    def kind(cut):
        return 0 if cut[3] == narrow else 1

    def first(cut, off):
        target = lax.rem(me + off, count)
        return remote(
            piece(target, cut), slot(d, r, cut), first_send.at[kind(cut)], first_recv.at[cut[2]],
            (q * GROUP + lax.rem(target, GROUP), c, target // GROUP),
        )

    def first_arrived(cut):
        row = pl.ds(0, count - 1)
        at = full_ref.at[0, row, :, pl.ds(cut[0], cut[1])] if cut[3] == narrow else half_ref.at[0, row]
        return remote(at, at, first_send.at[0], first_recv.at[cut[2]], (pr, c, d))

    def send_line(source_ref, dst_ref, block, cut, right):
        sems, place_ = (right_send, block) if right else (left_send, block - 1)
        return remote(
            source_ref, dst_ref, sems.at[block, kind(cut)], line_recv.at[place_, cut[2]],
            (r + GROUP if right else r - GROUP, c, d),
        )

    def along(block, cut, right):
        at = block_at(block, cut)
        return send_line(at, at, block, cut, right)

    def arrived(block, cut, right):
        at = block_at(block, cut)
        return remote(at, at, right_send.at[0, 0], line_recv.at[block if right else block - 1, cut[2]], (pr, c, d))

    def to_right(t):
        return (q + 1 < steps) & ((t < kept) | (q + 2 < steps))

    def to_left(t):
        return (q > 0) & ((t < kept) | (q > 1))

    def both(cut, source_ref, dst_ref):
        @pl.when(to_right(cut[2]))
        def _():
            send_line(source_ref, dst_ref, q, cut, True).start()

        @pl.when(to_left(cut[2]))
        def _():
            send_line(source_ref, dst_ref, q, cut, False).start()

    def give(n, sem, device, source_ref):
        return remote(source_ref, hid_ref.at[n, slice_], hid_send.at[sem], hid_recv.at[sem], device)

    cross = [give(1, 0, (pr, c, d), hidden_ref), None, give(3, 1, (pr, c, d), hid_ref.at[2, slice_])]
    far_hid = give(2, 2, (r + inward, c, d), hidden_ref)
    spread = [
        [give(n, 3 + n, device, hidden_ref if n == 0 else hid_ref.at[n, slice_]) for device in same] for n in range(2 * GROUP)
    ]

    def spread_all(n):
        at = hid_ref.at[n, pl.ds(0, len(same))]
        return remote(at, at, hid_send.at[3 + n], hid_recv.at[3 + n], (pr, c, d))

    pl.semaphore_wait(barrier, near + as_count(q + 1 < steps) + as_count(q > 0))

    @pl.when(end)
    def _():
        far_hid.start()

    def launch(cut):
        both(cut, piece(me, cut), slot(d, r, cut))
        for off in range(1, count):
            first(cut, off).start()

    loop(0, whole, lambda t: launch(span(t)))
    for cut in ends_of:
        launch(cut)

    cross[0].start()
    for copy in spread[0]:
        copy.start()

    has_head = ~((d > 0) & (j == 0))
    peer_head = ~((d > 0) & (pj == 0))
    has_tail = (d == depths - 1) & (j == GROUP - 1)
    peer_tail = (d == depths - 1) & (pj == GROUP - 1)
    shift = lay.shift * (depths - 1)

    def source(part, at, size):
        begin = jnp.clip(lay.stride * part - lay.shift * d + at, 0, lay.half - size)
        return teacher_ref.at[pl.ds(pl.multiple_of(begin, 16), size)]

    own_body = pltpu.make_async_copy(source(j, shift, lay.last - shift), own_ref.at[pl.ds(shift, lay.last - shift)], own_sem.at[3])
    own_head = pltpu.make_async_copy(source(j, 0, shift), own_ref.at[pl.ds(0, shift)], own_sem.at[4])
    own_tail = pltpu.make_async_copy(source(j, lay.last, shift), own_ref.at[pl.ds(lay.last, shift)], own_sem.at[5])
    own_hid = pltpu.make_async_copy(hidden_ref, hid_ref.at[0, slice_], own_sem.at[6])
    own_piece.start()
    own_half.start()
    own_hid.start()
    own_body.start()

    @pl.when(has_head)
    def _():
        own_head.start()

    @pl.when(has_tail)
    def _():
        own_tail.start()

    @pl.when(server)
    def _():
        far_hid.wait_recv()
        cross[2].start()
        for copy in spread[2]:
            copy.start()

    def start_line(cut):
        first_arrived(cut).wait_recv()
        for off in range(1, count):
            sender = lax.rem(me + count - off, count)
            at = slot(sender // GROUP, q * GROUP + lax.rem(sender, GROUP), cut)
            both(cut, at, at)

    loop(0, whole, lambda t: start_line(span(t)))
    for cut in ends_of:
        start_line(cut)

    body = lay.last - edge

    def teach_rows(index, at, size, sem=0):
        return remote(source(pj, at, size), other_ref.at[pl.ds(at, size)], teach_send.at[sem], teach_recv.at[index], (pr, c, d))

    def teach(t):
        return teach_rows(t, pl.multiple_of(t * CHUNK, CHUNK), CHUNK)

    teach_zero = teach_rows(0, shift, CHUNK - shift)
    teach_head = teach_rows(whole + 1, 0, shift, 1)
    teach_body = teach_rows(whole, edge, body)
    teach_tail = teach_rows(whole + 2, lay.last, shift, 2)

    def teach_kept():
        teach_zero.start()

        @pl.when(peer_head)
        def _():
            teach_head.start()

        loop(1, kept, lambda t: teach(t).start())

    def teach_rest():
        loop(kept, whole, lambda t: teach(t).start())
        teach_body.start()

        @pl.when(peer_tail)
        def _():
            teach_tail.start()

    @pl.when(end)
    def _():
        teach_rest()

    teach_kept()

    @pl.when(~end)
    def _():
        teach_rest()

    cross[0].wait_recv()
    for copy in spread[1]:
        copy.start()

    @pl.when(server)
    def _():
        cross[2].wait_recv()
        for copy in spread[3]:
            copy.start()

    def teach_end_arrived():
        teach_body.wait_recv()

        @pl.when(has_tail)
        def _():
            teach_tail.wait_recv()

    base = kept * CHUNK

    def extra_rows(n, index, at, size, sem=0):
        return remote(
            source(j, at, size) if n == 0 else other_ref.at[pl.ds(at, size)],
            extra_ref.at[n, pl.ds(at - base, size)], extra_send.at[sem], extra_recv.at[index], (r + inward, c, d),
        )

    def extra_arrived(index, at, size, sem=0):
        both_sets = extra_ref.at[:, pl.ds(at - base, size)]
        return remote(both_sets, both_sets, extra_send.at[sem], extra_recv.at[index], (pr, c, d))

    def extra_at(t):
        return t - kept, pl.multiple_of(t * CHUNK, CHUNK), CHUNK

    extra_body = (whole - kept, edge, body)
    extra_tail = (whole - kept + 1, lay.last, shift, 1)

    @pl.when(end)
    def _():
        def pass_on(t):
            teach(t).wait_recv()
            for n in range(GROUP):
                extra_rows(n, *extra_at(t)).start()

        loop(kept, whole, pass_on)
        teach_end_arrived()
        for n in range(GROUP):
            extra_rows(n, *extra_body).start()

        @pl.when(has_tail)
        def _():
            for n in range(GROUP):
                extra_rows(n, *extra_tail).start()

    def hop(k, cut):
        t = cut[2]
        wanted = (t < kept) | ~end

        @pl.when((q - k >= 0) & wanted)
        def _():
            arrived(q - k, cut, True).wait_recv()

            @pl.when(to_right(t))
            def _():
                along(q - k, cut, True).start()

        @pl.when((q + k < steps) & wanted)
        def _():
            arrived(q + k, cut, False).wait_recv()

            @pl.when(to_left(t))
            def _():
                along(q + k, cut, False).start()

    far = jnp.maximum(q, steps - 1 - q)

    def early(k):
        loop(0, whole, lambda t: hop(k, span(t)))
        for cut in ends_of:
            hop(k, cut)

    loop(1, far, early)

    for n in range(2 * GROUP):
        for k in range(5):
            acc[n, k] = jnp.full(acc.shape[2:], LOW if k in (0, 2) else 0.0, jnp.float32)

    def features(t):
        return full_ref[:, :, :, pl.ds(pl.multiple_of(t * CHUNK, CHUNK), CHUNK)].reshape(-1, CHUNK)

    def end_features():
        tile = full_ref[:, :, :, edge:].reshape(-1, lay.plain)
        half = half_ref[...]
        half = jnp.concatenate([half[..., : LANE // 2], half[..., LANE // 2 :]], axis=2).reshape(-1, LANE // 2)
        return jnp.concatenate([tile, half], axis=1)

    def main(rows_, at, valid=None):
        for n, ref in enumerate((own_ref, other_ref)):
            add_terms(rows_, hid_ref, acc, n, ref[at, :], valid)

    def more(rows_, at, valid=None):
        for n in range(GROUP):
            add_terms(rows_, hid_ref, acc, GROUP + n, extra_ref[n, at, :], valid)

    def rows_at(t):
        return pl.ds(pl.multiple_of(t * CHUNK, CHUNK), CHUNK)

    hop(far, span(0))
    own_body.wait()

    @pl.when(has_head)
    def _():
        own_head.wait()

    @pl.when(has_tail)
    def _():
        own_tail.wait()

    own_hid.wait()
    own_piece.wait()
    own_half.wait()
    for n in range(2):
        spread_all(n).wait_recv()
    teach_zero.wait_recv()

    @pl.when(has_head)
    def _():
        teach_head.wait_recv()

    main(features(0), rows_at(0), (jnp.where(has_head, 0, shift), CHUNK))

    def kept_chunk(t):
        hop(far, span(t))
        teach(t).wait_recv()
        main(features(t), rows_at(t))

    loop(1, kept, kept_chunk)

    @pl.when(server)
    def _():
        for n in range(2, 4):
            spread_all(n).wait_recv()

    @pl.when(~end)
    def _():
        def rest_chunk(t):
            hop(far, span(t))

            @pl.when(server)
            def _():
                extra_arrived(*extra_at(t)).wait_recv()
                more(features(t), rows_at(t - kept))

            teach(t).wait_recv()
            main(features(t), rows_at(t))

        loop(kept, whole, rest_chunk)
        for cut in ends_of:
            hop(far, cut)

    def close(n):
        values = merge([acc[n, k] for k in range(5)])
        stats_ref[n] = jnp.concatenate(values + [values[0]] * 3, axis=0)

    def tell(n, sem, device, source_set):
        return remote(stats_ref.at[source_set], held_ref.at[n], stats_send.at[sem], stats_recv.at[sem], device)

    def told(sem, begin, size):
        at = held_ref.at[pl.ds(begin, size)]
        return remote(at, at, stats_send.at[sem], stats_recv.at[sem], (pr, c, d))

    limit = (0, jnp.where(j == 0, lay.stride, lay.last + lay.shift * d) - edge)

    @pl.when(server)
    def _():
        extra_arrived(*extra_body).wait_recv()

        @pl.when(has_tail)
        def _():
            extra_arrived(*extra_tail).wait_recv()

        more(end_features(), pl.ds(edge - base, lay.rest), limit)
        for n in range(GROUP, 2 * GROUP):
            close(n)
        for n, (a, b, e, dj) in enumerate(group):
            tell(near + n, 1, (a - inward, b, e), GROUP + dj).start()

    @pl.when(~end)
    def _():
        teach_end_arrived()
        main(end_features(), pl.ds(edge, lay.rest), limit)

    for n in range(GROUP):
        close(n)
    for n, (a, b, e, dj) in enumerate(peers):
        tell(n, 0, (a, b, e), dj).start()

    @pl.when(~end)
    def _():
        for n in range(len(group)):
            for k in range(5):
                held_ref[near + n, k] = jnp.full(held_ref.shape[2:], LOW if k in (0, 2) else 0.0, jnp.float32)

    def settle(block):
        def sent(right, size):
            at = block_at(block, (0, size, 0, narrow))
            remote(at, at, (right_send if right else left_send).at[block, 0], line_recv.at[0, 0], (pr, c, d)).wait_send()

        def sent_half(right):
            at = block_at(block, ends_of[1])
            remote(at, at, (right_send if right else left_send).at[block, 1], line_recv.at[0, 0], (pr, c, d)).wait_send()

        @pl.when((block <= q) & (q + 2 < steps))
        def _():
            sent(True, lay.stride)
            sent_half(True)

        @pl.when((block <= q) & (q + 2 == steps))
        def _():
            sent(True, base)

        @pl.when((block >= q) & (q > 1))
        def _():
            sent(False, lay.stride)
            sent_half(False)

        @pl.when((block >= q) & (q == 1))
        def _():
            sent(False, base)

    loop(0, steps, settle)
    sent_pieces = full_ref.at[0, pl.ds(0, count - 1)]
    remote(sent_pieces, sent_pieces, first_send.at[0], first_recv.at[0], (pr, c, d)).wait_send()
    sent_halves = half_ref.at[0, pl.ds(0, count - 1)]
    remote(sent_halves, sent_halves, first_send.at[1], first_recv.at[0], (pr, c, d)).wait_send()
    cross[0].wait_send()
    for n in range(2):
        spread_all(n).wait_send()
    taught = other_ref.at[pl.ds(shift, lay.last - shift)]
    remote(taught, taught, teach_send.at[0], teach_recv.at[0], (pr, c, d)).wait_send()

    @pl.when(peer_head)
    def _():
        teach_head.wait_send()

    @pl.when(peer_tail)
    def _():
        teach_tail.wait_send()

    @pl.when(end)
    def _():
        far_hid.wait_send()
        extra_arrived(0, base, lay.last - base).wait_send()

        @pl.when(has_tail)
        def _():
            extra_arrived(*extra_tail).wait_send()

    @pl.when(server)
    def _():
        cross[2].wait_send()
        for n in range(2, 4):
            spread_all(n).wait_send()
        told(1, near, len(group)).wait_send()

    told(0, 0, near).wait()

    @pl.when(end)
    def _():
        told(1, near, len(group)).wait_recv()

    blocks = [stats_ref[0]] + [held_ref[n] for n in range(near + len(group))]
    parts = [jnp.concatenate([block[k : k + 1] for block in blocks], axis=0) for k in range(5)]
    peak, total, _, teacher_total, cross_sum = merge(parts)
    sums_ref[...] = jnp.concatenate([peak, total, teacher_total, cross_sum] + [peak] * 4, axis=0)


def on_device(rows, cols, depths, student_hidden, embedding, teacher_logits):
    vocab, narrow = embedding.shape
    lay = Layout(vocab, depths)
    hidden = student_hidden.T
    features, tokens = hidden.shape
    steps = rows // GROUP
    slots = 2 * GROUP * cols * depths - 1
    whole, height = lay.whole, lay.edge + lay.rest
    dma = pltpu.SemaphoreType.DMA
    any_space = pl.BlockSpec(memory_space=pl.ANY)
    dtype = embedding.dtype
    sums = pl.pallas_call(
        functools.partial(kernel, rows, cols, depths, lay),
        out_shape=jax.ShapeDtypeStruct((8, tokens), jnp.float32),
        in_specs=[any_space] * 3,
        out_specs=pl.BlockSpec(memory_space=pltpu.VMEM),
        scratch_shapes=[
            pltpu.VMEM((narrow, vocab), dtype),
            pltpu.VMEM((depths * GROUP, narrow // 2, LANE), dtype),
            pltpu.VMEM((depths, rows, narrow, lay.stride), dtype),
            pltpu.VMEM((depths, rows, narrow // 2, LANE), dtype),
            pltpu.VMEM((height, tokens), teacher_logits.dtype),
            pltpu.VMEM((height, tokens), teacher_logits.dtype),
            pltpu.VMEM((GROUP, height - lay.kept * CHUNK, tokens), teacher_logits.dtype),
            pltpu.VMEM((2 * GROUP, depths * cols, features, tokens), hidden.dtype),
            pltpu.VMEM((2 * GROUP, 5, 8, tokens), jnp.float32),
            pltpu.VMEM((2 * GROUP, 8, tokens), jnp.float32),
            pltpu.VMEM((slots, 8, tokens), jnp.float32),
            dma((7,)), dma((2,)), dma((whole + 2,)), dma((steps, 2)), dma((steps, 2)), dma((steps - 1, whole + 2)),
            dma((3,)), dma((whole + 3,)), dma((2,)), dma((whole - lay.kept + 2,)),
            dma((3 + 2 * GROUP,)), dma((3 + 2 * GROUP,)), dma((2,)), dma((2,)),
        ],
        compiler_params=pltpu.CompilerParams(collective_id=0, has_side_effects=True, vmem_limit_bytes=60 * 2**20),
        name="distill",
    )(embedding.T, teacher_logits.T, hidden)
    norm_log = jnp.log(sums[1])
    return sums[0] + norm_log - sums[3] / sums[2], -norm_log


def solution(mesh):
    sizes = [mesh.shape[name] for name in ("row", "col", "depth")]
    in_specs = (P("row", ("depth", "col")), P("col", ("depth", "row")), P("row", ("col", "depth")))
    out_specs = (P("row"), P("row"))
    return jax.shard_map(
        functools.partial(on_device, *sizes), mesh=mesh, in_specs=in_specs, out_specs=out_specs, check_vma=False
    )
```

time: 122 us -> 121 us (level)
    pallas_call x1, Pallas kernels: 120 us -> 119 us  [on_device(): pl.pallas_call(functools.partial(kernel, rows, cols, depths, lay), out_sh...]
where the time goes in v3:
time: 121 us
  Pallas kernels  119 us (98%)
  other arithmetic  1.42 us (1%)
    pallas_call x1, Pallas kernels, on_device(): pl.pallas_call(functools.partial(kernel, rows, cols, depths, lay), out_sh...  119 us

profile of v3, /device:TPU:0, one launch (start us, length us, event | category | flops | bytes accessed | tf_op | source)
XLA Modules:
  0.0 120.9 jit_solution(3662983470694640734)
XLA Ops:
  0.6 118.8 %distill.1 = f32[8,256]{1,0:T(8,128)} custom-call(bf16[48,25152]{1,0:T(8,128)(2,1)} %bitcast.6, bf16[12576,256]{1,0:T(8,128)(2,1)} %bitcast.5, bf16[192,256]{1,0:T(8,128)(2,1)} %bitcast.7), custom_call_target="tpu_custom_call" | custom-call | tf_op jit(solution)/shard_map/distill/pallas_call | solution.py:624
  119.5 1.4 %fusion = (f32[1,256]{1,0:T(1,128)}, f32[1,256]{1,0:T(1,128)}) fusion(f32[8,256]{1,0:T(8,128)} %distill.1), kind=kLoop, calls=%fused_computation.2 | loop fusion | flops 1024 | bytes 6144 | tf_op jit(solution)/shard_map/neg | solution.py:649

commit v4 on v3

--- a/solution.py
+++ b/solution.py
@@ -10,8 +10,8 @@
 MESH = pl.DeviceIdType.MESH
 GROUP = 2
 LANE = 128
-CHUNK = 512
-KEPT = 0.64
+CHUNK = 384
+KEPT = 0.67
 LOW = -1e30
 
 
@@ -54,47 +54,55 @@
     lax.fori_loop(begin, stop, step, 0)
 
 
-def merge(parts):
+def gather_terms(parts):
     top, total, teacher_top, teacher_total, cross = parts
     peak = jnp.max(top, axis=0, keepdims=True)
     teacher_peak = jnp.max(teacher_top, axis=0, keepdims=True)
     scale = jnp.exp(teacher_top - teacher_peak)
+    weight = jnp.sum(teacher_total * scale, axis=0, keepdims=True)
     return [
         peak,
         jnp.sum(total * jnp.exp(top - peak), axis=0, keepdims=True),
-        teacher_peak,
-        jnp.sum(teacher_total * scale, axis=0, keepdims=True),
-        jnp.sum(cross * scale, axis=0, keepdims=True),
+        teacher_peak + jnp.log(weight),
+        jnp.sum(cross * scale, axis=0, keepdims=True) / weight,
     ]
 
 
-def add_terms(rows, hid_ref, acc, n, teacher, valid=None):
-    size = rows.shape[1]
-    hidden = hid_ref[n].reshape(rows.shape[0], -1)
-    tokens = hidden.shape[1]
-    student = lax.dot_general(rows, hidden, (((0,), (0,)), ((), ())), preferred_element_type=jnp.float32)
+def fold(values):
+    whole = jnp.concatenate(values, axis=0)
+    half = whole.shape[1] // 2
+    return jnp.concatenate([whole[:, :half], whole[:, half:]], axis=0)
+
+
+def product(rows, hidden):
+    return lax.dot_general(rows, hidden, (((0,), (0,)), ((), ())), preferred_element_type=jnp.float32)
+
+
+def add_terms(student, acc, at, teacher, valid=None):
+    size = student.shape[0]
     teacher = teacher.astype(jnp.float32)
     if valid is not None:
         index = lax.broadcasted_iota(jnp.int32, student.shape, 0)
         keep = (index >= valid[0]) & (index < valid[1])
         student = jnp.where(keep, student, LOW)
         teacher = jnp.where(keep, teacher, LOW)
-    student = student.reshape(size // 8, 8, tokens)
-    teacher = teacher.reshape(size // 8, 8, tokens)
-    top = jnp.maximum(acc[n, 0], jnp.max(student, axis=0))
-    acc[n, 1] = acc[n, 1] * jnp.exp(acc[n, 0] - top) + jnp.sum(jnp.exp(student - top[None]), axis=0)
-    acc[n, 0] = top
-    teacher_top = jnp.maximum(acc[n, 2], jnp.max(teacher, axis=0))
-    fade = jnp.exp(acc[n, 2] - teacher_top)
+    student = student.reshape(size // 8, 8, -1)
+    teacher = teacher.reshape(size // 8, 8, -1)
+    old, teacher_old = acc[0, :, at], acc[2, :, at]
+    top = jnp.maximum(old, jnp.max(student, axis=0))
+    acc[1, :, at] = acc[1, :, at] * jnp.exp(old - top) + jnp.sum(jnp.exp(student - top[None]), axis=0)
+    acc[0, :, at] = top
+    teacher_top = jnp.maximum(teacher_old, jnp.max(teacher, axis=0))
+    fade = jnp.exp(teacher_old - teacher_top)
     weights = jnp.exp(teacher - teacher_top[None])
-    acc[n, 3] = acc[n, 3] * fade + jnp.sum(weights, axis=0)
-    acc[n, 4] = acc[n, 4] * fade + jnp.sum(weights * student, axis=0)
-    acc[n, 2] = teacher_top
+    acc[3, :, at] = acc[3, :, at] * fade + jnp.sum(weights, axis=0)
+    acc[4, :, at] = acc[4, :, at] * fade + jnp.sum(weights * student, axis=0)
+    acc[2, :, at] = teacher_top
 
 
 def kernel(
     rows, cols, depths, lay, emb_ref, teacher_ref, hidden_ref, sums_ref,
-    table_ref, pack_ref, full_ref, half_ref, own_ref, other_ref, extra_ref, hid_ref, acc, stats_ref, held_ref,
+    table_ref, pack_ref, full_ref, half_ref, own_ref, other_ref, extra_ref, hid_ref, acc, ahead_ref, stats_ref, held_ref,
     own_sem, first_send, first_recv, right_send, left_send, line_recv, teach_send, teach_recv, extra_send, extra_recv,
     hid_send, hid_recv, stats_send, stats_recv,
 ):
@@ -105,6 +113,7 @@
     kept, whole, edge = lay.kept, lay.whole, lay.edge
     narrow = table_ref.shape[0]
     packed = narrow // 2
+    tokens = hidden_ref.shape[1]
     end, server, inward = ends(rows, q)
     pj = lax.rem(j + 1, GROUP)
     pr = q * GROUP + pj
@@ -218,17 +227,20 @@
         def _():
             send_line(source_ref, dst_ref, q, cut, False).start()
 
+    def hidden_at(n, where=None):
+        return hid_ref.at[slice_ if where is None else where, :, pl.ds(n * tokens, tokens)]
+
     def give(n, sem, device, source_ref):
-        return remote(source_ref, hid_ref.at[n, slice_], hid_send.at[sem], hid_recv.at[sem], device)
-
-    cross = [give(1, 0, (pr, c, d), hidden_ref), None, give(3, 1, (pr, c, d), hid_ref.at[2, slice_])]
+        return remote(source_ref, hidden_at(n), hid_send.at[sem], hid_recv.at[sem], device)
+
+    cross = [give(1, 0, (pr, c, d), hidden_ref), None, give(3, 1, (pr, c, d), hidden_at(2))]
     far_hid = give(2, 2, (r + inward, c, d), hidden_ref)
     spread = [
-        [give(n, 3 + n, device, hidden_ref if n == 0 else hid_ref.at[n, slice_]) for device in same] for n in range(2 * GROUP)
+        [give(n, 3 + n, device, hidden_ref if n == 0 else hidden_at(n)) for device in same] for n in range(2 * GROUP)
     ]
 
     def spread_all(n):
-        at = hid_ref.at[n, pl.ds(0, len(same))]
+        at = hidden_at(n, pl.ds(0, len(same)))
         return remote(at, at, hid_send.at[3 + n], hid_recv.at[3 + n], (pr, c, d))
 
     pl.semaphore_wait(barrier, near + as_count(q + 1 < steps) + as_count(q > 0))
@@ -263,7 +275,7 @@
     own_body = pltpu.make_async_copy(source(j, shift, lay.last - shift), own_ref.at[pl.ds(shift, lay.last - shift)], own_sem.at[3])
     own_head = pltpu.make_async_copy(source(j, 0, shift), own_ref.at[pl.ds(0, shift)], own_sem.at[4])
     own_tail = pltpu.make_async_copy(source(j, lay.last, shift), own_ref.at[pl.ds(lay.last, shift)], own_sem.at[5])
-    own_hid = pltpu.make_async_copy(hidden_ref, hid_ref.at[0, slice_], own_sem.at[6])
+    own_hid = pltpu.make_async_copy(hidden_ref, hidden_at(0), own_sem.at[6])
     own_piece.start()
     own_half.start()
     own_hid.start()
@@ -416,26 +428,68 @@
 
     loop(1, far, early)
 
-    for n in range(2 * GROUP):
-        for k in range(5):
-            acc[n, k] = jnp.full(acc.shape[2:], LOW if k in (0, 2) else 0.0, jnp.float32)
+    for k in range(5):
+        acc[k] = jnp.full(acc.shape[1:], LOW if k in (0, 2) else 0.0, jnp.float32)
 
     def features(t):
         return full_ref[:, :, :, pl.ds(pl.multiple_of(t * CHUNK, CHUNK), CHUNK)].reshape(-1, CHUNK)
 
-    def end_features():
-        tile = full_ref[:, :, :, edge:].reshape(-1, lay.plain)
-        half = half_ref[...]
-        half = jnp.concatenate([half[..., : LANE // 2], half[..., LANE // 2 :]], axis=2).reshape(-1, LANE // 2)
-        return jnp.concatenate([tile, half], axis=1)
+    def token_lanes(sets):
+        return pl.ds(sets[0] * tokens, len(sets) * tokens)
+
+    def hidden_of(sets):
+        return hid_ref[:, :, token_lanes(sets)].reshape(-1, len(sets) * tokens)
+
+    def unpacked(half):
+        half = jnp.concatenate([half[..., : LANE // 2], half[..., LANE // 2 :]], axis=2)
+        return half.reshape(-1, LANE // 2)
+
+    def tile_features(block=None):
+        at = pl.ds(0, rows) if block is None else pl.ds(block * GROUP, GROUP)
+        return full_ref[:, at, :, edge:].reshape(-1, lay.plain)
+
+    def half_features(block=None):
+        return unpacked(half_ref[:, pl.ds(0, rows) if block is None else pl.ds(block * GROUP, GROUP)])
+
+    def hidden_block(block, sets):
+        begin = block * (GROUP * narrow)
+        at = pl.ds(pl.multiple_of(lax.rem(begin, hid_ref.shape[1]), 16), GROUP * narrow)
+        parts = [hid_ref[depth * cols + begin // hid_ref.shape[1], at, token_lanes(sets)] for depth in range(depths)]
+        return jnp.concatenate(parts, axis=0)
 
     def main(rows_, at, valid=None):
         for n, ref in enumerate((own_ref, other_ref)):
-            add_terms(rows_, hid_ref, acc, n, ref[at, :], valid)
-
-    def more(rows_, at, valid=None):
+            add_terms(product(rows_, hidden_of((n,))), acc, token_lanes((n,)), ref[at, :], valid)
+
+    def more(rows_, at):
         for n in range(GROUP):
-            add_terms(rows_, hid_ref, acc, GROUP + n, extra_ref[n, at, :], valid)
+            add_terms(product(rows_, hidden_of((GROUP + n,))), acc, token_lanes((GROUP + n,)), extra_ref[n, at, :])
+
+    def teacher_of(sets, begin, size):
+        at = pl.ds(begin, size)
+        own = [own_ref[at, :], other_ref[at, :]]
+        taken = [extra_ref[n, pl.ds(begin - base, size), :] for n in range(GROUP)] if len(sets) > GROUP else []
+        return jnp.concatenate(own + taken, axis=1)
+
+    ahead = steps <= 4 and narrow % 32 == 16 and hid_ref.shape[1] % (GROUP * narrow) == 0
+    last_block = jnp.where(q * 2 < steps, steps - 1, 0)
+
+    def prepare(sets):
+        if not ahead:
+            return
+        tile = half = None
+        for n in range(1, steps):
+            block = lax.rem(last_block + n, steps)
+            hidden = hidden_block(block, sets)
+            tile_part, half_part = product(tile_features(block), hidden), product(half_features(block), hidden)
+            tile, half = (tile_part, half_part) if tile is None else (tile + tile_part, half + half_part)
+        ahead_ref[pl.ds(0, lay.plain), token_lanes(sets)] = tile
+        ahead_ref[pl.ds(lay.plain, LANE // 2), token_lanes(sets)] = half
+
+    def end_student(sets, take, begin, size):
+        if not ahead:
+            return product(take(), hidden_of(sets))
+        return ahead_ref[pl.ds(begin, size), token_lanes(sets)] + product(take(last_block), hidden_block(last_block, sets))
 
     def rows_at(t):
         return pl.ds(pl.multiple_of(t * CHUNK, CHUNK), CHUNK)
@@ -481,21 +535,31 @@
         def rest_chunk(t):
             hop(far, span(t))
 
+            teach(t).wait_recv()
+            main(features(t), rows_at(t))
+
             @pl.when(server)
             def _():
                 extra_arrived(*extra_at(t)).wait_recv()
                 more(features(t), rows_at(t - kept))
 
-            teach(t).wait_recv()
-            main(features(t), rows_at(t))
-
-        loop(kept, whole, rest_chunk)
-        for cut in ends_of:
-            hop(far, cut)
-
-    def close(n):
-        values = merge([acc[n, k] for k in range(5)])
-        stats_ref[n] = jnp.concatenate(values + [values[0]] * 3, axis=0)
+        loop(kept, whole - 1, rest_chunk)
+
+        @pl.when(server)
+        def _():
+            prepare(tuple(range(2 * GROUP)))
+
+        @pl.when(~server)
+        def _():
+            prepare(tuple(range(GROUP)))
+
+        rest_chunk(whole - 1)
+
+    def close(sets):
+        at = pl.ds(sets[0] * tokens, len(sets) * tokens)
+        values = gather_terms([acc[k, :, at] for k in range(5)])
+        for n in range(len(sets)):
+            stats_ref[sets[n]] = fold([value[:, n * tokens : (n + 1) * tokens] for value in values])
 
     def tell(n, sem, device, source_set):
         return remote(stats_ref.at[source_set], held_ref.at[n], stats_send.at[sem], stats_recv.at[sem], device)
@@ -504,7 +568,32 @@
         at = held_ref.at[pl.ds(begin, size)]
         return remote(at, at, stats_send.at[sem], stats_recv.at[sem], (pr, c, d))
 
-    limit = (0, jnp.where(j == 0, lay.stride, lay.last + lay.shift * d) - edge)
+    limit = (0, lay.last + lay.shift * d - lay.stride)
+    half_used = j == GROUP - 1
+
+    own_sets, all_sets = tuple(range(GROUP)), tuple(range(2 * GROUP))
+
+    def tell_near():
+        for n, (a, b, e, dj) in reversed(list(enumerate(peers))):
+            tell(n, 0, (a, b, e), dj).start()
+
+    def finish(sets):
+        at = token_lanes(sets)
+        student = end_student(sets, tile_features, 0, lay.plain)
+        add_terms(student, acc, at, teacher_of(sets, edge, lay.plain))
+        hop(far, ends_of[1])
+
+        @pl.when(half_used)
+        def _():
+            student = end_student(sets, half_features, lay.plain, LANE // 2)
+            add_terms(student, acc, at, teacher_of(sets, lay.stride, LANE // 2), limit)
+
+        close(sets)
+
+    @pl.when(~end)
+    def _():
+        hop(far, ends_of[0])
+        teach_end_arrived()
 
     @pl.when(server)
     def _():
@@ -514,27 +603,25 @@
         def _():
             extra_arrived(*extra_tail).wait_recv()
 
-        more(end_features(), pl.ds(edge - base, lay.rest), limit)
-        for n in range(GROUP, 2 * GROUP):
-            close(n)
-        for n, (a, b, e, dj) in enumerate(group):
+        finish(all_sets)
+        for n, (a, b, e, dj) in reversed(list(enumerate(group))):
             tell(near + n, 1, (a - inward, b, e), GROUP + dj).start()
 
+    @pl.when(~end & ~server)
+    def _():
+        finish(own_sets)
+
+    @pl.when(end)
+    def _():
+        close(own_sets)
+
+    tell_near()
+
     @pl.when(~end)
     def _():
-        teach_end_arrived()
-        main(end_features(), pl.ds(edge, lay.rest), limit)
-
-    for n in range(GROUP):
-        close(n)
-    for n, (a, b, e, dj) in enumerate(peers):
-        tell(n, 0, (a, b, e), dj).start()
-
-    @pl.when(~end)
-    def _():
+        kinds = lax.broadcasted_iota(jnp.int32, held_ref.shape[1:], 0) % 2
         for n in range(len(group)):
-            for k in range(5):
-                held_ref[near + n, k] = jnp.full(held_ref.shape[2:], LOW if k in (0, 2) else 0.0, jnp.float32)
+            held_ref[near + n] = jnp.where(kinds == 0, LOW, 0.0)
 
     def settle(block):
         def sent(right, size):
@@ -605,9 +692,12 @@
         told(1, near, len(group)).wait_recv()
 
     blocks = [stats_ref[0]] + [held_ref[n] for n in range(near + len(group))]
-    parts = [jnp.concatenate([block[k : k + 1] for block in blocks], axis=0) for k in range(5)]
-    peak, total, _, teacher_total, cross_sum = merge(parts)
-    sums_ref[...] = jnp.concatenate([peak, total, teacher_total, cross_sum] + [peak] * 4, axis=0)
+    top = functools.reduce(jnp.maximum, blocks)
+    scales = [jnp.exp(block - top) for block in blocks]
+    weight = functools.reduce(jnp.add, scales)
+    scaled = functools.reduce(jnp.add, [block * pltpu.roll(scale, 1, 0) for block, scale in zip(blocks, scales)])
+    row_kind = lax.broadcasted_iota(jnp.int32, top.shape, 0) % 4
+    sums_ref[...] = jnp.where(row_kind == 0, top, jnp.where(row_kind == 2, weight, scaled))
 
 
 def on_device(rows, cols, depths, student_hidden, embedding, teacher_logits):
@@ -623,7 +713,7 @@
     dtype = embedding.dtype
     sums = pl.pallas_call(
         functools.partial(kernel, rows, cols, depths, lay),
-        out_shape=jax.ShapeDtypeStruct((8, tokens), jnp.float32),
+        out_shape=jax.ShapeDtypeStruct((8, tokens // 2), jnp.float32),
         in_specs=[any_space] * 3,
         out_specs=pl.BlockSpec(memory_space=pltpu.VMEM),
         scratch_shapes=[
@@ -634,19 +724,21 @@
             pltpu.VMEM((height, tokens), teacher_logits.dtype),
             pltpu.VMEM((height, tokens), teacher_logits.dtype),
             pltpu.VMEM((GROUP, height - lay.kept * CHUNK, tokens), teacher_logits.dtype),
-            pltpu.VMEM((2 * GROUP, depths * cols, features, tokens), hidden.dtype),
-            pltpu.VMEM((2 * GROUP, 5, 8, tokens), jnp.float32),
-            pltpu.VMEM((2 * GROUP, 8, tokens), jnp.float32),
-            pltpu.VMEM((slots, 8, tokens), jnp.float32),
+            pltpu.VMEM((depths * cols, features, 2 * GROUP * tokens), hidden.dtype),
+            pltpu.VMEM((5, 8, 2 * GROUP * tokens), jnp.float32),
+            pltpu.VMEM((lay.rest, 2 * GROUP * tokens), jnp.float32),
+            pltpu.VMEM((2 * GROUP, 8, tokens // 2), jnp.float32),
+            pltpu.VMEM((slots, 8, tokens // 2), jnp.float32),
             dma((7,)), dma((2,)), dma((whole + 2,)), dma((steps, 2)), dma((steps, 2)), dma((steps - 1, whole + 2)),
             dma((3,)), dma((whole + 3,)), dma((2,)), dma((whole - lay.kept + 2,)),
             dma((3 + 2 * GROUP,)), dma((3 + 2 * GROUP,)), dma((2,)), dma((2,)),
         ],
-        compiler_params=pltpu.CompilerParams(collective_id=0, has_side_effects=True, vmem_limit_bytes=60 * 2**20),
+        compiler_params=pltpu.CompilerParams(collective_id=0, has_side_effects=True, vmem_limit_bytes=54 * 2**20 - 84 * 2**10),
         name="distill",
     )(embedding.T, teacher_logits.T, hidden)
-    norm_log = jnp.log(sums[1])
-    return sums[0] + norm_log - sums[3] / sums[2], -norm_log
+    peak, total, weight, cross = (sums.reshape(2, 4, -1)[:, k].reshape(-1) for k in range(4))
+    norm_log = jnp.log(total)
+    return peak + norm_log - cross / weight, -norm_log
 
 
 def solution(mesh):

time: 121 us -> 119 us (0.983)
  no operation moved by 1% of the time
where the time goes in v4:
time: 119 us
  Pallas kernels  118 us (99%)
    pallas_call x1, Pallas kernels, on_device(): pl.pallas_call(functools.partial(kernel, rows, cols, depths, lay), out_sh...  118 us

profile of v4, /device:TPU:0, one launch (start us, length us, event | category | flops | bytes accessed | tf_op | source)
XLA Modules:
  0.0 119.0 jit_solution(13532554299690310924)
XLA Ops:
  0.6 117.8 %distill.1 = f32[8,128]{1,0:T(8,128)S(1)} custom-call(bf16[48,25152]{1,0:T(8,128)(2,1)} %bitcast.8, bf16[12576,256]{1,0:T(8,128)(2,1)} %bitcast.7, bf16[192,256]{1,0:T(8,128)(2,1)} %bitcast.9), custom_call_target="tpu_custom_call" | custom-call | tf_op jit(solution)/shard_map/distill/pallas_call | solution.py:714
  118.4 0.6 fusion.1

commit v5 on v4

--- a/solution.py
+++ b/solution.py
@@ -21,9 +21,10 @@
         self.stride = vocab // LANE // (depths * GROUP) * LANE
         self.shift = self.half - GROUP * self.stride
         self.last = self.half - (GROUP - 1) * self.stride
-        self.edge = (self.stride - LANE) // CHUNK * CHUNK
+        self.edge = ((self.stride - LANE) // CHUNK - 1) * CHUNK
         self.whole = self.edge // CHUNK
         self.plain = self.stride - self.edge
+        self.tiles = self.plain // LANE
         self.rest = self.plain + LANE // 2
         self.kept = round(self.stride / CHUNK * KEPT)
         assert depths == 2 and 0 <= self.shift < CHUNK and self.shift % 16 == 0
@@ -159,7 +160,11 @@
     def span(t):
         return pl.multiple_of(t * CHUNK, CHUNK), CHUNK, t, narrow
 
-    ends_of = ((edge, lay.plain, whole, narrow), (lay.stride, LANE, whole + 1, packed))
+    def tile_span(i):
+        return pl.multiple_of(edge + i * LANE, LANE), LANE, whole + i, narrow
+
+    half_span = (lay.stride, LANE, whole + lay.tiles, packed)
+    ends_of = tuple(tile_span(i) for i in range(lay.tiles)) + (half_span,)
 
     def piece(target, cut):
         first_lane, size, index, height = cut
@@ -180,7 +185,7 @@
         table_ref.at[:, pl.ds(pl.multiple_of(lay.stride * me, LANE), lay.stride)],
         full_ref.at[d, r], own_sem.at[1],
     )
-    own_half = pltpu.make_async_copy(pack_ref.at[me], slot(d, r, ends_of[1]), own_sem.at[2])
+    own_half = pltpu.make_async_copy(pack_ref.at[me], slot(d, r, half_span), own_sem.at[2])
 
     def kind(cut):
         return 0 if cut[3] == narrow else 1
@@ -303,9 +308,6 @@
             at = slot(sender // GROUP, q * GROUP + lax.rem(sender, GROUP), cut)
             both(cut, at, at)
 
-    loop(0, whole, lambda t: start_line(span(t)))
-    for cut in ends_of:
-        start_line(cut)
 
     body = lay.last - edge
 
@@ -337,6 +339,8 @@
         def _():
             teach_tail.start()
 
+    loop(0, whole * 3 // 4, lambda t: start_line(span(t)))
+
     @pl.when(end)
     def _():
         teach_rest()
@@ -346,6 +350,10 @@
     @pl.when(~end)
     def _():
         teach_rest()
+
+    loop(whole * 3 // 4, whole, lambda t: start_line(span(t)))
+    for cut in ends_of:
+        start_line(cut)
 
     cross[0].wait_recv()
     for copy in spread[1]:
@@ -444,9 +452,9 @@
         half = jnp.concatenate([half[..., : LANE // 2], half[..., LANE // 2 :]], axis=2)
         return half.reshape(-1, LANE // 2)
 
-    def tile_features(block=None):
+    def tile_features(begin, size, block=None):
         at = pl.ds(0, rows) if block is None else pl.ds(block * GROUP, GROUP)
-        return full_ref[:, at, :, edge:].reshape(-1, lay.plain)
+        return full_ref[:, at, :, pl.ds(begin, size)].reshape(-1, size)
 
     def half_features(block=None):
         return unpacked(half_ref[:, pl.ds(0, rows) if block is None else pl.ds(block * GROUP, GROUP)])
@@ -468,7 +476,7 @@
     def teacher_of(sets, begin, size):
         at = pl.ds(begin, size)
         own = [own_ref[at, :], other_ref[at, :]]
-        taken = [extra_ref[n, pl.ds(begin - base, size), :] for n in range(GROUP)] if len(sets) > GROUP else []
+        taken = [extra_ref[n, pl.ds(pl.multiple_of(begin - base, LANE // 2), size), :] for n in range(GROUP)] if len(sets) > GROUP else []
         return jnp.concatenate(own + taken, axis=1)
 
     ahead = steps <= 4 and narrow % 32 == 16 and hid_ref.shape[1] % (GROUP * narrow) == 0
@@ -477,14 +485,15 @@
     def prepare(sets):
         if not ahead:
             return
-        tile = half = None
+        at = token_lanes(sets)
+        tiles, half_rows = pl.ds(0, lay.plain), pl.ds(lay.plain, LANE // 2)
         for n in range(1, steps):
             block = lax.rem(last_block + n, steps)
             hidden = hidden_block(block, sets)
-            tile_part, half_part = product(tile_features(block), hidden), product(half_features(block), hidden)
-            tile, half = (tile_part, half_part) if tile is None else (tile + tile_part, half + half_part)
-        ahead_ref[pl.ds(0, lay.plain), token_lanes(sets)] = tile
-        ahead_ref[pl.ds(lay.plain, LANE // 2), token_lanes(sets)] = half
+            tile = product(tile_features(edge, lay.plain, block), hidden)
+            half = product(half_features(block), hidden)
+            ahead_ref[tiles, at] = tile if n == 1 else ahead_ref[tiles, at] + tile
+            ahead_ref[half_rows, at] = half if n == 1 else ahead_ref[half_rows, at] + half
 
     def end_student(sets, take, begin, size):
         if not ahead:
@@ -579,9 +588,16 @@
 
     def finish(sets):
         at = token_lanes(sets)
-        student = end_student(sets, tile_features, 0, lay.plain)
-        add_terms(student, acc, at, teacher_of(sets, edge, lay.plain))
-        hop(far, ends_of[1])
+
+        def tile_terms(i):
+            cut = tile_span(i)
+            hop(far, cut)
+            take = functools.partial(tile_features, cut[0], LANE)
+            student = end_student(sets, take, pl.multiple_of(i * LANE, LANE), LANE)
+            add_terms(student, acc, at, teacher_of(sets, cut[0], LANE))
+
+        loop(0, lay.tiles, tile_terms)
+        hop(far, half_span)
 
         @pl.when(half_used)
         def _():
@@ -592,7 +608,6 @@
 
     @pl.when(~end)
     def _():
-        hop(far, ends_of[0])
         teach_end_arrived()
 
     @pl.when(server)
@@ -629,7 +644,7 @@
             remote(at, at, (right_send if right else left_send).at[block, 0], line_recv.at[0, 0], (pr, c, d)).wait_send()
 
         def sent_half(right):
-            at = block_at(block, ends_of[1])
+            at = block_at(block, half_span)
             remote(at, at, (right_send if right else left_send).at[block, 1], line_recv.at[0, 0], (pr, c, d)).wait_send()
 
         @pl.when((block <= q) & (q + 2 < steps))
@@ -729,7 +744,7 @@
             pltpu.VMEM((lay.rest, 2 * GROUP * tokens), jnp.float32),
             pltpu.VMEM((2 * GROUP, 8, tokens // 2), jnp.float32),
             pltpu.VMEM((slots, 8, tokens // 2), jnp.float32),
-            dma((7,)), dma((2,)), dma((whole + 2,)), dma((steps, 2)), dma((steps, 2)), dma((steps - 1, whole + 2)),
+            dma((7,)), dma((2,)), dma((whole + lay.tiles + 1,)), dma((steps, 2)), dma((steps, 2)), dma((steps - 1, whole + lay.tiles + 1)),
             dma((3,)), dma((whole + 3,)), dma((2,)), dma((whole - lay.kept + 2,)),
             dma((3 + 2 * GROUP,)), dma((3 + 2 * GROUP,)), dma((2,)), dma((2,)),
         ],

time: 119 us -> 118 us (level)
  no operation moved by 1% of the time
where the time goes in v5:
time: 118 us
  Pallas kernels  117 us (99%)
    pallas_call x1, Pallas kernels, on_device(): pl.pallas_call(functools.partial(kernel, rows, cols, depths, lay), out_sh...  117 us

profile of v5, /device:TPU:0, one launch (start us, length us, event | category | flops | bytes accessed | tf_op | source)
XLA Modules:
  0.0 118.3 jit_solution(10556840096433351159)
XLA Ops:
  0.6 117.1 %distill.1 = f32[8,128]{1,0:T(8,128)S(1)} custom-call(bf16[48,25152]{1,0:T(8,128)(2,1)} %bitcast.8, bf16[12576,256]{1,0:T(8,128)(2,1)} %bitcast.7, bf16[192,256]{1,0:T(8,128)(2,1)} %bitcast.9), custom_call_target="tpu_custom_call" | custom-call | tf_op jit(solution)/shard_map/distill/pallas_call | solution.py:729
  117.7 0.6 fusion.1
